TPU v7x, 32 devices: a whole 2x2x4 slice. The times are simulated.
32 devices in a mesh: head: 2 (over core), blk: 4 (over z), rep: 4 (over y, x).
Axes of the slice: x: 2, y: 2, z: 4, core: 2. Of those that a mesh axis runs over, the one named last changes fastest.
Arguments:
- queries: bfloat16 [2048, 768], P(('blk', 'rep'), 'head'), may hold values from -400 to 400
- keys: bfloat16 [2048, 256], P(('blk', 'rep'), 'head'), may hold values from -6 to 6
- values: bfloat16 [2048, 256], P(('blk', 'rep'), 'head'), may hold values from -18 to 18
- stretch_order: int32 [16], replicated, may hold values from 0 to 15, each once
- out_weight: bfloat16 [768, 3072], P('head'), may hold values from -0.21875 to 0.21875
Outputs:
- mixed_rows: bfloat16 [2048, 3072], P(('blk', 'rep'), 'head')
- log_sum_exp: float32 [6, 2048], P('head', ('blk', 'rep'))
Inputs may be any that keep to these rules, and one draw needn't show every extreme that they name: `stretch_order`: each stretch number appears once.
All inputs are finite; a program needn't handle non-finite values.
Results may differ from a plain program's by a relative error of at most 0.02.
Values may be sent and summed in bfloat16 or wider, within the bound.
No kernel may reach another device: no remote copies, remote signals or barrier semaphores. Data moves between devices by JAX's collectives and lax.ppermute only.
A program may use at most 128 MiB of HBM per device.

v0:
```python
import math

import jax
import jax.numpy as jnp
from jax import lax
from jax.experimental import pallas as pl
from jax.experimental.pallas import tpu as pltpu
from jax.sharding import PartitionSpec as P


GROUP = 3
DH = 128
NEG_FILL = -1e30
LOG2E = math.log2(math.e)
STAT_ROWS = 16
OUT_STEP = 512


VMEM = pl.BlockSpec(memory_space=pltpu.VMEM)
HBM = pl.BlockSpec(memory_space=pltpu.HBM)


def source_of(me, hop, count):
    if count & (count - 1) == 0:
        return lax.bitwise_xor(me, jnp.int32(hop))
    return lax.rem(me + (count - hop), count)


def hops_out(hop, count):
    if count & (count - 1) == 0:
        return [(i, i ^ hop) for i in range(count)]
    return [(i, (i + hop) % count) for i in range(count)]


def hops_back(hop, count):
    return [(b, a) for a, b in hops_out(hop, count)]


def pack_kernel(
    spans, span_len, query_hbm, keys_hbm, values_hbm, order_hbm,
    query_ref, packed_ref, bound_ref, values_ref, order_ref, sems,
):
    tok = values_ref.shape[0]
    heads, kv_heads = query_ref.shape[0] // tok, packed_ref.shape[0]
    order_copy = pltpu.make_async_copy(order_hbm, order_ref, sems.at[0])
    value_copy = pltpu.make_async_copy(values_hbm, values_ref, sems.at[1])
    copies = []
    for head in range(kv_heads):
        copies.append((keys_hbm.at[:, pl.ds(head * DH, DH)], packed_ref.at[head, 0]))
    for head in range(heads):
        copies.append(
            (query_hbm.at[:, pl.ds(head * DH, DH)], query_ref.at[pl.ds(head * tok, tok), :])
        )
    copies = [
        pltpu.make_async_copy(source, target, sems.at[2 + at])
        for at, (source, target) in enumerate(copies)
    ]
    value_copy.start()
    order_copy.start()
    for copy in copies:
        copy.start()
    value_copy.wait()
    for head in range(kv_heads):
        packed_ref[head, 1] = values_ref[:, head * DH : (head + 1) * DH].T
    order_copy.wait()
    blk_rank, rep_rank = lax.axis_index("blk"), lax.axis_index("rep")
    for rep_hop in range(span_len):
        query_at = blk_rank * span_len + source_of(rep_rank, rep_hop, span_len)
        for hop in range(spans):
            key_at = source_of(blk_rank, hop, spans) * span_len + rep_rank
            row = rep_hop * spans + hop
            bound_ref[row : row + 1, :] = jnp.full(
                (1, tok), (order_ref[query_at] - order_ref[key_at]) * tok, jnp.int32
            )
    for copy in copies:
        copy.wait()


def attend_kernel(rep_hop, spans, bound_ref, query_ref, *refs):
    kv_refs, out_ref = refs[:spans], refs[spans]
    tok = bound_ref.shape[1]
    kv_heads = kv_refs[0].shape[0]
    factor = DH**-0.5
    lanes = GROUP * tok
    ahead = lax.broadcasted_iota(jnp.int32, (tok, tok), 0) - lax.broadcasted_iota(
        jnp.int32, (tok, tok), 1
    )
    ahead = jnp.concatenate([ahead] * GROUP, axis=1)
    for kv_head in range(kv_heads):
        rows = slice(kv_head * lanes, (kv_head + 1) * lanes)
        query = query_ref[rows, :]
        scores = []
        for hop in range(spans):
            raw = lax.dot_general(
                kv_refs[hop][kv_head, 0],
                query,
                (((1,), (1,)), ((), ())),
                preferred_element_type=jnp.float32,
            )
            at = rep_hop * spans + hop
            bound = jnp.concatenate([bound_ref[at : at + 1, :]] * GROUP, axis=1)
            scores.append(jnp.where(ahead <= bound, raw, NEG_FILL))
        top = scores[0]
        for hop in range(1, spans):
            top = jnp.maximum(top, scores[hop])
        top = jnp.max(top, axis=0, keepdims=True)
        weight_sum, numer = None, None
        for hop in range(spans):
            weights = jnp.exp2((scores[hop] - top) * (factor * LOG2E))
            weight_sum = weights if weight_sum is None else weight_sum + weights
            term = lax.dot_general(
                kv_refs[hop][kv_head, 1],
                weights.astype(jnp.bfloat16),
                (((1,), (0,)), ((), ())),
                preferred_element_type=jnp.float32,
            )
            numer = term if numer is None else numer + term
        total = jnp.sum(weight_sum, axis=0, keepdims=True)
        out_ref[0:DH, rows] = (numer * (1.0 / total)).astype(jnp.bfloat16)
        log_sum = top * factor + jnp.log(total)
        high = log_sum.astype(jnp.bfloat16)
        rest = log_sum - high.astype(jnp.float32)
        middle = rest.astype(jnp.bfloat16)
        low = (rest - middle.astype(jnp.float32)).astype(jnp.bfloat16)
        out_ref[DH : DH + STAT_ROWS, rows] = jnp.concatenate(
            [high, middle, low, jnp.zeros((STAT_ROWS - 3, lanes), jnp.bfloat16)], axis=0
        )


def attend_fetch_kernel(spans, chunks, *refs):
    weight_hbm, part_ref, weight_ref, sems = refs[-4:]
    rows, width = weight_ref.shape[0] // chunks, weight_ref.shape[1]
    columns = pl.ds(pl.multiple_of(lax.axis_index("head") * width, 128), width)
    copies = []
    for chunk in range(chunks):
        here = pl.ds(chunk * rows, rows)
        copies.append(
            pltpu.make_async_copy(
                weight_hbm.at[here, columns], weight_ref.at[here, :], sems.at[chunk]
            )
        )
        copies[-1].start()
    attend_kernel(0, spans, *refs[:-4], part_ref)
    for copy in copies:
        copy.wait()


def combine_kernel(*refs):
    part_refs, (attended_ref, log_sum_ref) = refs[:-2], refs[-2:]
    stats = []
    for part in part_refs:
        parts = part[DH : DH + STAT_ROWS, :].astype(jnp.float32)
        stats.append(parts[0:1] + parts[1:2] + parts[2:3])
    top = stats[0]
    for stat in stats[1:]:
        top = jnp.maximum(top, stat)
    shares = [jnp.exp(stat - top) for stat in stats]
    total = shares[0]
    for share in shares[1:]:
        total = total + share
    scale = 1.0 / total
    numer = None
    for part, share in zip(part_refs, shares):
        term = part[0:DH, :].astype(jnp.float32) * (share * scale)
        numer = term if numer is None else numer + term
    attended_ref[...] = numer.astype(jnp.bfloat16)
    log_sum = top + jnp.log(total)
    tok = log_sum_ref.shape[1]
    for head in range(log_sum_ref.shape[0]):
        log_sum_ref[head : head + 1, :] = log_sum[:, head * tok : (head + 1) * tok]


def project(attended_ref, weight_ref, tok, columns):
    out = None
    for head in range(weight_ref.shape[0] // DH):
        term = lax.dot_general(
            attended_ref[:, head * tok : (head + 1) * tok],
            weight_ref[head * DH : (head + 1) * DH, columns],
            (((0,), (0,)), ((), ())),
            preferred_element_type=jnp.float32,
        )
        out = term if out is None else out + term
    return out.astype(jnp.bfloat16)


def project_home_kernel(attended_ref, weight_ref, out_ref):
    out_ref[...] = project(attended_ref, weight_ref, out_ref.shape[0], slice(None))


def finish_kernel(
    home_ref, other_ref, weight_ref, log_ref, out_hbm, log_hbm, out_ref, sems
):
    tok, width = out_ref.shape
    log_copy = pltpu.make_async_copy(log_ref, log_hbm, sems.at[0])
    log_copy.start()
    step = math.gcd(width, OUT_STEP)
    base = lax.axis_index("head") * width
    copies = [log_copy]
    for at in range(width // step):
        here = slice(at * step, (at + 1) * step)
        columns = pl.ds(pl.multiple_of(base + at * step, 128), step)
        other = project(other_ref, weight_ref, tok, columns)
        out_ref[:, here] = (
            home_ref[:, here].astype(jnp.float32) + other.astype(jnp.float32)
        ).astype(jnp.bfloat16)
        copies.append(
            pltpu.make_async_copy(
                out_ref.at[:, here], out_hbm.at[:, here], sems.at[1 + at]
            )
        )
        copies[-1].start()
    for copy in copies:
        copy.wait()


def cost(flops, moved, transcendentals=0):
    return pl.CostEstimate(flops=flops, bytes_accessed=moved, transcendentals=transcendentals)


def in_hbm(array):
    return pltpu.with_memory_space_constraint(array, pltpu.HBM)


def params(mib):
    return pltpu.CompilerParams(vmem_limit_bytes=mib * 2**20)


def body(queries, keys, values, stretch_order, out_weight):
    tok = queries.shape[0]
    kv_heads = keys.shape[1] // DH
    heads = kv_heads * GROUP
    width = out_weight.shape[1] // lax.axis_size("head")
    spans, span_len = lax.axis_size("blk"), lax.axis_size("rep")
    query, packed, bounds = pl.pallas_call(
        lambda *refs: pack_kernel(spans, span_len, *refs),
        out_shape=(
            jax.ShapeDtypeStruct((heads * tok, DH), jnp.bfloat16),
            jax.ShapeDtypeStruct((kv_heads, 2, tok, DH), jnp.bfloat16),
            jax.ShapeDtypeStruct((spans * span_len, tok), jnp.int32),
        ),
        in_specs=[HBM] * 4,
        out_specs=(VMEM, VMEM, VMEM),
        scratch_shapes=[
            pltpu.VMEM((tok, kv_heads * DH), jnp.bfloat16),
            pltpu.SMEM(stretch_order.shape, jnp.int32),
            pltpu.SemaphoreType.DMA((2 + kv_heads + heads,)),
        ],
        compiler_params=params(4),
        name="pack",
    )(*[in_hbm(x) for x in (queries, keys, values, stretch_order)])
    kv, query = [packed], [query]
    for hop in range(1, spans):
        kv.append(lax.ppermute(packed, "blk", hops_out(hop, spans)))
    for hop in range(1, span_len):
        query.append(lax.ppermute(query[0], "rep", hops_out(hop, span_len)))
    weight_away = lax.ppermute(out_weight, "head", [(0, 1), (1, 0)])
    part_shape = jax.ShapeDtypeStruct((DH + STAT_ROWS, heads * tok), jnp.bfloat16)
    attend = dict(
        cost_estimate=cost(
            4 * heads * tok * spans * tok * DH,
            2 * heads * tok * DH * 2 + spans * tok * DH * 4,
            heads * tok * spans * tok,
        ),
        compiler_params=params(16 if spans > 8 else 8),
    )
    chunks = heads * DH // math.gcd(heads * DH, 64)
    parts = [None]
    for hop in range(1, span_len):
        parts.append(
            pl.pallas_call(
                lambda *refs, hop=hop: attend_kernel(hop, spans, *refs),
                out_shape=part_shape,
                in_specs=[VMEM] * (2 + spans),
                out_specs=VMEM,
                name="attend",
                **attend,
            )(bounds, query[hop], *kv)
        )
    parts[0], weight = pl.pallas_call(
        lambda *refs: attend_fetch_kernel(spans, chunks, *refs),
        out_shape=(part_shape, jax.ShapeDtypeStruct((heads * DH, width), jnp.bfloat16)),
        in_specs=[VMEM] * (2 + spans) + [HBM],
        out_specs=(VMEM, VMEM),
        scratch_shapes=[pltpu.SemaphoreType.DMA((chunks,))],
        name="attend_fetch",
        **attend,
    )(bounds, query[0], *kv, in_hbm(out_weight))
    returned = [parts[0]]
    for hop in range(1, span_len):
        returned.append(lax.ppermute(parts[hop], "rep", hops_back(hop, span_len)))
    attended, log_sum = pl.pallas_call(
        combine_kernel,
        out_shape=(
            jax.ShapeDtypeStruct((DH, heads * tok), jnp.bfloat16),
            jax.ShapeDtypeStruct((heads, tok), jnp.float32),
        ),
        in_specs=[VMEM] * span_len,
        out_specs=(VMEM, VMEM),
        compiler_params=params(4),
        name="combine",
    )(*returned)
    other = lax.ppermute(attended, "head", [(0, 1), (1, 0)])
    shape = jax.ShapeDtypeStruct((tok, width), jnp.bfloat16)
    home = pl.pallas_call(
        project_home_kernel,
        out_shape=shape,
        in_specs=[VMEM, VMEM],
        out_specs=VMEM,
        cost_estimate=cost(2 * tok * heads * DH * width, heads * DH * width * 2),
        compiler_params=params(4),
        name="project_home",
    )(attended, weight)
    return pl.pallas_call(
        finish_kernel,
        out_shape=(shape, jax.ShapeDtypeStruct((heads, tok), jnp.float32)),
        in_specs=[VMEM, VMEM, VMEM, VMEM],
        out_specs=(HBM, HBM),
        scratch_shapes=[
            pltpu.VMEM((tok, width), jnp.bfloat16),
            pltpu.SemaphoreType.DMA((1 + width // math.gcd(width, OUT_STEP),)),
        ],
        compiler_params=params(4),
        name="finish",
    )(home, other, weight_away, log_sum)


def solution(mesh):
    in_specs = (
        P(("blk", "rep"), "head"),
        P(("blk", "rep"), "head"),
        P(("blk", "rep"), "head"),
        P(),
        P("head", None),
    )
    out_specs = (P(("blk", "rep"), "head"), P("head", ("blk", "rep")))

    return jax.shard_map(body, mesh=mesh, in_specs=in_specs, out_specs=out_specs, check_vma=False)
```

profile of v0, /device:TPU:0, one launch (start us, length us, event | category | flops | bytes accessed | tf_op | source)
XLA Modules:
  0.0 30.7 jit_solution(15397799618261728145)
XLA Ops:
  0.6 0.6 %collective-permute-start.10 = (bf16[384,3072]{1,0:T(8,128)(2,1)}, bf16[384,3072]{1,0:T(8,128)(2,1)S(1)}, u32[]{:S(2)}, u32[]{:S(2)}) collective-permute-start(bf16[384,3072]{1,0:T(8,128)(2,1)} %refs_6_.1), channel_id=1, source_target_pairs={{0,16},{16,0},{1,17},{17,1},{2,18},{18,2},{3,19},{19,3},{4,20},{20... | collective-permute-start | bytes 7077896 | tf_op jit(solution)/shard_map/ppermute | solution.py:256
  1.2 0.9 %pack.1 = (bf16[384,128]{1,0:T(8,128)(2,1)S(1)}, bf16[1,2,128,128]{3,2,1,0:T(8,128)(2,1)S(1)}, s32[16,128]{1,0:T(8,128)S(1)}) custom-call(bf16[128,384]{1,0:T(8,128)(2,1)} %refs_0_.1, bf16[128,128]{1,0:T(8,128)(2,1)} %refs_1_.1, bf16[128,128]{1,0:T(8,128)(2,1)} %refs_2_.1, s32[16]{0:T(128)} %refs_3_.1), custom_call_target="tpu_custom_call" | custom-call | tf_op jit(solution)/shard_map/pack/pallas_call | solution.py:234
  2.1 4.7 %collective-permute-start.2 = (bf16[1,2,128,128]{3,2,1,0:T(8,128)(2,1)S(1)}, bf16[1,2,128,128]{3,2,1,0:T(8,128)(2,1)S(1)}, u32[]{:S(2)}, u32[]{:S(2)}) collective-permute-start(bf16[1,2,128,128]{3,2,1,0:T(8,128)(2,1)S(1)} %get-tuple-element.11.refs_2_), channel_id=1, source_target_pairs={{0,12},{4,8},{8,4},{12,0},{1,13},{5,9},{9,5},{13,1},{2,14},{6,10},... | collective-permute-start | bytes 196616 | tf_op jit(solution)/shard_map/ppermute | solution.py:253
  6.8 0.0 collective-permute-start.1
  6.8 1.5 %collective-permute-start.3 = (bf16[384,128]{1,0:T(8,128)(2,1)S(1)}, bf16[384,128]{1,0:T(8,128)(2,1)S(1)}, u32[]{:S(2)}, u32[]{:S(2)}) collective-permute-start(bf16[384,128]{1,0:T(8,128)(2,1)S(1)} %get-tuple-element.10.refs_1_), channel_id=1, source_target_pairs={{0,1},{1,0},{2,3},{3,2},{4,5},{5,4},{6,7},{7,6},{8,9},{9,8},{10,11... | collective-permute-start | bytes 294920 | tf_op jit(solution)/shard_map/ppermute | solution.py:255
  8.3 1.5 %collective-permute-start.5 = (bf16[384,128]{1,0:T(8,128)(2,1)S(1)}, bf16[384,128]{1,0:T(8,128)(2,1)S(1)}, u32[]{:S(2)}, u32[]{:S(2)}) collective-permute-start(bf16[384,128]{1,0:T(8,128)(2,1)S(1)} %get-tuple-element.10.refs_1_), channel_id=1, source_target_pairs={{0,2},{1,3},{2,0},{3,1},{4,6},{5,7},{6,4},{7,5},{8,10},{9,11},{10,... | collective-permute-start | bytes 294920 | tf_op jit(solution)/shard_map/ppermute | solution.py:255
  9.8 2.4 %collective-permute-start.7 = (bf16[384,128]{1,0:T(8,128)(2,1)S(1)}, bf16[384,128]{1,0:T(8,128)(2,1)S(1)}, u32[]{:S(2)}, u32[]{:S(2)}) collective-permute-start(bf16[384,128]{1,0:T(8,128)(2,1)S(1)} %get-tuple-element.10.refs_1_), channel_id=1, source_target_pairs={{0,3},{1,2},{2,1},{3,0},{4,7},{5,6},{6,5},{7,4},{8,11},{9,10},{10,... | collective-permute-start | bytes 294920 | tf_op jit(solution)/shard_map/ppermute | solution.py:255
  12.2 0.7 %collective-permute-done.1.refs_4_ = bf16[1,2,128,128]{3,2,1,0:T(8,128)(2,1)S(1)} collective-permute-done((bf16[1,2,128,128]{3,2,1,0:T(8,128)(2,1)S(1)}, bf16[1,2,128,128]{3,2,1,0:T(8,128)(2,1)S(1)}, u32[]{:S(2)}, u32[]{:S(2)}) %collective-permute-start.1) | collective-permute-done | bytes 65568 | tf_op jit(solution)/shard_map/ppermute | solution.py:253
  12.9 2.1 %collective-permute-start = (bf16[1,2,128,128]{3,2,1,0:T(8,128)(2,1)S(1)}, bf16[1,2,128,128]{3,2,1,0:T(8,128)(2,1)S(1)}, u32[]{:S(2)}, u32[]{:S(2)}) collective-permute-start(bf16[1,2,128,128]{3,2,1,0:T(8,128)(2,1)S(1)} %get-tuple-element.11.refs_2_), channel_id=1, source_target_pairs={{0,4},{4,0},{8,12},{12,8},{1,5},{5,1},{9,13},{13,9},{2,6},{6,2},{1... | collective-permute-start | bytes 196616 | tf_op jit(solution)/shard_map/ppermute | solution.py:253
  15.0 2.2 %collective-permute-done.refs_3_ = bf16[1,2,128,128]{3,2,1,0:T(8,128)(2,1)S(1)} collective-permute-done((bf16[1,2,128,128]{3,2,1,0:T(8,128)(2,1)S(1)}, bf16[1,2,128,128]{3,2,1,0:T(8,128)(2,1)S(1)}, u32[]{:S(2)}, u32[]{:S(2)}) %collective-permute-start) | collective-permute-done | bytes 65568 | tf_op jit(solution)/shard_map/ppermute | solution.py:253
  17.2 0.7 %attend.3 = bf16[144,384]{1,0:T(8,128)(2,1)S(1)} custom-call(s32[16,128]{1,0:T(8,128)S(1)} %get-tuple-element.9.refs_0_, bf16[384,128]{1,0:T(8,128)(2,1)S(1)} %collective-permute-done.3.refs_1_, bf16[1,2,128,128]{3,2,1,0:T(8,128)(2,1)S(1)} %get-tuple-element.11.refs_2_, bf16[1,2,128,128]{3,2,1,0:T(8,128)(2,1)S(1)} %collective-permute-done.refs_3_, ...), custom_call_target="tpu_custom_call" | custom-call | flops 100663296 | bytes 458752 | tf_op jit(solution)/shard_map/attend/pallas_call | solution.py:270
  17.9 1.5 %collective-permute-start.4 = (bf16[144,384]{1,0:T(8,128)(2,1)S(1)}, bf16[144,384]{1,0:T(8,128)(2,1)S(1)}, u32[]{:S(2)}, u32[]{:S(2)}) collective-permute-start(bf16[144,384]{1,0:T(8,128)(2,1)S(1)} %attend.3), channel_id=1, source_target_pairs={{1,0},{0,1},{3,2},{2,3},{5,4},{4,5},{7,6},{6,7},{9,8},{8,9},{11,10... | collective-permute-start | bytes 331784 | tf_op jit(solution)/shard_map/ppermute | solution.py:290
  19.4 0.7 %attend.4 = bf16[144,384]{1,0:T(8,128)(2,1)S(1)} custom-call(s32[16,128]{1,0:T(8,128)S(1)} %get-tuple-element.9.refs_0_, bf16[384,128]{1,0:T(8,128)(2,1)S(1)} %collective-permute-done.5.refs_1_, bf16[1,2,128,128]{3,2,1,0:T(8,128)(2,1)S(1)} %get-tuple-element.11.refs_2_, bf16[1,2,128,128]{3,2,1,0:T(8,128)(2,1)S(1)} %collective-permute-done.refs_3_, ...), custom_call_target="tpu_custom_call" | custom-call | flops 100663296 | bytes 458752 | tf_op jit(solution)/shard_map/attend/pallas_call | solution.py:270
  20.1 1.6 %collective-permute-start.6 = (bf16[144,384]{1,0:T(8,128)(2,1)S(1)}, bf16[144,384]{1,0:T(8,128)(2,1)S(1)}, u32[]{:S(2)}, u32[]{:S(2)}) collective-permute-start(bf16[144,384]{1,0:T(8,128)(2,1)S(1)} %attend.4), channel_id=1, source_target_pairs={{2,0},{3,1},{0,2},{1,3},{6,4},{7,5},{4,6},{5,7},{10,8},{11,9},{8,1... | collective-permute-start | bytes 331784 | tf_op jit(solution)/shard_map/ppermute | solution.py:290
  21.6 0.7 %attend.5 = bf16[144,384]{1,0:T(8,128)(2,1)S(1)} custom-call(s32[16,128]{1,0:T(8,128)S(1)} %get-tuple-element.9.refs_0_, bf16[384,128]{1,0:T(8,128)(2,1)S(1)} %collective-permute-done.7.refs_1_, bf16[1,2,128,128]{3,2,1,0:T(8,128)(2,1)S(1)} %get-tuple-element.11.refs_2_, bf16[1,2,128,128]{3,2,1,0:T(8,128)(2,1)S(1)} %collective-permute-done.refs_3_, ...), custom_call_target="tpu_custom_call" | custom-call | flops 100663296 | bytes 458752 | tf_op jit(solution)/shard_map/attend/pallas_call | solution.py:270
  22.3 0.6 %collective-permute-start.8 = (bf16[144,384]{1,0:T(8,128)(2,1)S(1)}, bf16[144,384]{1,0:T(8,128)(2,1)S(1)}, u32[]{:S(2)}, u32[]{:S(2)}) collective-permute-start(bf16[144,384]{1,0:T(8,128)(2,1)S(1)} %attend.5), channel_id=1, source_target_pairs={{3,0},{2,1},{1,2},{0,3},{7,4},{6,5},{5,6},{4,7},{11,8},{10,9},{9,1... | collective-permute-start | bytes 331784 | tf_op jit(solution)/shard_map/ppermute | solution.py:290
  22.9 1.9 %attend_fetch.1 = (bf16[144,384]{1,0:T(8,128)(2,1)S(1)}, bf16[384,1536]{1,0:T(8,128)(2,1)S(1)}) custom-call(s32[16,128]{1,0:T(8,128)S(1)} %get-tuple-element.9.refs_0_, bf16[384,128]{1,0:T(8,128)(2,1)S(1)} %get-tuple-element.10.refs_1_, bf16[1,2,128,128]{3,2,1,0:T(8,128)(2,1)S(1)} %get-tuple-element.11.refs_2_, ...), custom_call_target="tpu_custom_call" | custom-call | flops 100663296 | bytes 458752 | tf_op jit(solution)/shard_map/attend_fetch/pallas_call | solution.py:279
  24.8 1.3 %collective-permute-done.6.refs_2_ = bf16[144,384]{1,0:T(8,128)(2,1)S(1)} collective-permute-done((bf16[144,384]{1,0:T(8,128)(2,1)S(1)}, bf16[144,384]{1,0:T(8,128)(2,1)S(1)}, u32[]{:S(2)}, u32[]{:S(2)}) %collective-permute-start.6) | collective-permute-done | bytes 110624 | tf_op jit(solution)/shard_map/ppermute | solution.py:290
  26.1 2.0 %collective-permute-done.8.refs_3_ = bf16[144,384]{1,0:T(8,128)(2,1)S(1)} collective-permute-done((bf16[144,384]{1,0:T(8,128)(2,1)S(1)}, bf16[144,384]{1,0:T(8,128)(2,1)S(1)}, u32[]{:S(2)}, u32[]{:S(2)}) %collective-permute-start.8) | collective-permute-done | bytes 110624 | tf_op jit(solution)/shard_map/ppermute | solution.py:290
  28.0 0.1 combine.1
  28.1 0.1 collective-permute-start.9
  28.2 0.5 %project_home.1.home_ref = bf16[128,1536]{1,0:T(8,128)(2,1)S(1)} custom-call(bf16[128,384]{1,0:T(8,128)(2,1)S(1)} %get-tuple-element.13.attended_ref, bf16[384,1536]{1,0:T(8,128)(2,1)S(1)} %get-tuple-element.14.weight_ref), custom_call_target="tpu_custom_call" | custom-call | flops 150994944 | bytes 1179648 | tf_op jit(solution)/shard_map/project_home/pallas_call | solution.py:304
  28.7 0.8 %collective-permute-done.9.other_ref = bf16[128,384]{1,0:T(8,128)(2,1)S(1)} collective-permute-done((bf16[128,384]{1,0:T(8,128)(2,1)S(1)}, bf16[128,384]{1,0:T(8,128)(2,1)S(1)}, u32[]{:S(2)}, u32[]{:S(2)}) %collective-permute-start.9) | collective-permute-done | bytes 98336 | tf_op jit(solution)/shard_map/ppermute | solution.py:302
  29.5 1.2 %finish.1 = (bf16[128,1536]{1,0:T(8,128)(2,1)}, f32[3,128]{1,0:T(4,128)}) custom-call(bf16[128,1536]{1,0:T(8,128)(2,1)S(1)} %project_home.1.home_ref, bf16[128,384]{1,0:T(8,128)(2,1)S(1)} %collective-permute-done.9.other_ref, bf16[384,3072]{1,0:T(8,128)(2,1)S(1)} %collective-permute-done.10.weight_ref, f32[3,128]{1,0:T(4,128)S(1)} %get-tuple-element.15.log_ref), custom_call_target="tpu_custom_call" | custom-call | tf_op jit(solution)/shard_map/finish/pallas_call | solution.py:313
  (6 shorter events, 0.0 us)
Async XLA Ops:
  0.6 28.9 %collective-permute-start.10 = (bf16[384,3072]{1,0:T(8,128)(2,1)}, bf16[384,3072]{1,0:T(8,128)(2,1)S(1)}, u32[]{:S(2)}, u32[]{:S(2)}) collective-permute-start(bf16[384,3072]{1,0:T(8,128)(2,1)} %refs_6_.1), channel_id=1, source_target_pairs={{0,16},{16,0},{1,17},{17,1},{2,18},{18,2},{3,19},{19,3},{4,20},{20... | collective-permute-start | bytes 7077896 | tf_op jit(solution)/shard_map/ppermute | solution.py:256
  2.1 7.7 %collective-permute-start.2 = (bf16[1,2,128,128]{3,2,1,0:T(8,128)(2,1)S(1)}, bf16[1,2,128,128]{3,2,1,0:T(8,128)(2,1)S(1)}, u32[]{:S(2)}, u32[]{:S(2)}) collective-permute-start(bf16[1,2,128,128]{3,2,1,0:T(8,128)(2,1)S(1)} %get-tuple-element.11.refs_2_), channel_id=1, source_target_pairs={{0,12},{4,8},{8,4},{12,0},{1,13},{5,9},{9,5},{13,1},{2,14},{6,10},... | collective-permute-start | bytes 196616 | tf_op jit(solution)/shard_map/ppermute | solution.py:253
  6.8 6.1 %collective-permute-start.1 = (bf16[1,2,128,128]{3,2,1,0:T(8,128)(2,1)S(1)}, bf16[1,2,128,128]{3,2,1,0:T(8,128)(2,1)S(1)}, u32[]{:S(2)}, u32[]{:S(2)}) collective-permute-start(bf16[1,2,128,128]{3,2,1,0:T(8,128)(2,1)S(1)} %get-tuple-element.11.refs_2_), channel_id=1, source_target_pairs={{0,8},{4,12},{8,0},{12,4},{1,9},{5,13},{9,1},{13,5},{2,10},{6,14},... | collective-permute-start | bytes 196616 | tf_op jit(solution)/shard_map/ppermute | solution.py:253
  6.8 10.4 %collective-permute-start.3 = (bf16[384,128]{1,0:T(8,128)(2,1)S(1)}, bf16[384,128]{1,0:T(8,128)(2,1)S(1)}, u32[]{:S(2)}, u32[]{:S(2)}) collective-permute-start(bf16[384,128]{1,0:T(8,128)(2,1)S(1)} %get-tuple-element.10.refs_1_), channel_id=1, source_target_pairs={{0,1},{1,0},{2,3},{3,2},{4,5},{5,4},{6,7},{7,6},{8,9},{9,8},{10,11... | collective-permute-start | bytes 294920 | tf_op jit(solution)/shard_map/ppermute | solution.py:255
  8.3 11.1 %collective-permute-start.5 = (bf16[384,128]{1,0:T(8,128)(2,1)S(1)}, bf16[384,128]{1,0:T(8,128)(2,1)S(1)}, u32[]{:S(2)}, u32[]{:S(2)}) collective-permute-start(bf16[384,128]{1,0:T(8,128)(2,1)S(1)} %get-tuple-element.10.refs_1_), channel_id=1, source_target_pairs={{0,2},{1,3},{2,0},{3,1},{4,6},{5,7},{6,4},{7,5},{8,10},{9,11},{10,... | collective-permute-start | bytes 294920 | tf_op jit(solution)/shard_map/ppermute | solution.py:255
  9.8 11.8 %collective-permute-start.7 = (bf16[384,128]{1,0:T(8,128)(2,1)S(1)}, bf16[384,128]{1,0:T(8,128)(2,1)S(1)}, u32[]{:S(2)}, u32[]{:S(2)}) collective-permute-start(bf16[384,128]{1,0:T(8,128)(2,1)S(1)} %get-tuple-element.10.refs_1_), channel_id=1, source_target_pairs={{0,3},{1,2},{2,1},{3,0},{4,7},{5,6},{6,5},{7,4},{8,11},{9,10},{10,... | collective-permute-start | bytes 294920 | tf_op jit(solution)/shard_map/ppermute | solution.py:255
  12.9 4.3 %collective-permute-start = (bf16[1,2,128,128]{3,2,1,0:T(8,128)(2,1)S(1)}, bf16[1,2,128,128]{3,2,1,0:T(8,128)(2,1)S(1)}, u32[]{:S(2)}, u32[]{:S(2)}) collective-permute-start(bf16[1,2,128,128]{3,2,1,0:T(8,128)(2,1)S(1)} %get-tuple-element.11.refs_2_), channel_id=1, source_target_pairs={{0,4},{4,0},{8,12},{12,8},{1,5},{5,1},{9,13},{13,9},{2,6},{6,2},{1... | collective-permute-start | bytes 196616 | tf_op jit(solution)/shard_map/ppermute | solution.py:253
  17.9 6.9 %collective-permute-start.4 = (bf16[144,384]{1,0:T(8,128)(2,1)S(1)}, bf16[144,384]{1,0:T(8,128)(2,1)S(1)}, u32[]{:S(2)}, u32[]{:S(2)}) collective-permute-start(bf16[144,384]{1,0:T(8,128)(2,1)S(1)} %attend.3), channel_id=1, source_target_pairs={{1,0},{0,1},{3,2},{2,3},{5,4},{4,5},{7,6},{6,7},{9,8},{8,9},{11,10... | collective-permute-start | bytes 331784 | tf_op jit(solution)/shard_map/ppermute | solution.py:290
  20.1 6.0 %collective-permute-start.6 = (bf16[144,384]{1,0:T(8,128)(2,1)S(1)}, bf16[144,384]{1,0:T(8,128)(2,1)S(1)}, u32[]{:S(2)}, u32[]{:S(2)}) collective-permute-start(bf16[144,384]{1,0:T(8,128)(2,1)S(1)} %attend.4), channel_id=1, source_target_pairs={{2,0},{3,1},{0,2},{1,3},{6,4},{7,5},{4,6},{5,7},{10,8},{11,9},{8,1... | collective-permute-start | bytes 331784 | tf_op jit(solution)/shard_map/ppermute | solution.py:290
  22.3 5.7 %collective-permute-start.8 = (bf16[144,384]{1,0:T(8,128)(2,1)S(1)}, bf16[144,384]{1,0:T(8,128)(2,1)S(1)}, u32[]{:S(2)}, u32[]{:S(2)}) collective-permute-start(bf16[144,384]{1,0:T(8,128)(2,1)S(1)} %attend.5), channel_id=1, source_target_pairs={{3,0},{2,1},{1,2},{0,3},{7,4},{6,5},{5,6},{4,7},{11,8},{10,9},{9,1... | collective-permute-start | bytes 331784 | tf_op jit(solution)/shard_map/ppermute | solution.py:290
  28.1 1.4 %collective-permute-start.9 = (bf16[128,384]{1,0:T(8,128)(2,1)S(1)}, bf16[128,384]{1,0:T(8,128)(2,1)S(1)}, u32[]{:S(2)}, u32[]{:S(2)}) collective-permute-start(bf16[128,384]{1,0:T(8,128)(2,1)S(1)} %get-tuple-element.13.attended_ref), channel_id=1, source_target_pairs={{0,16},{16,0},{1,17},{17,1},{2,18},{18,2},{3,19},{19,3},{4,20},{20... | collective-permute-start | bytes 294920 | tf_op jit(solution)/shard_map/ppermute | solution.py:302
where the time goes:
time: 30.9 us; the launch traced here: 30.7 us
  starting transfers between devices  16.4 us (53%)
  waiting for transfers between devices  6.99 us (23%)
  Pallas kernels  6.58 us (21%)
  between operations  0.7 us (2%)
    ppermute x3, starting transfers between devices, body(): kv.append(lax.ppermute(packed, 'blk', hops_out(hop, spans)))  6.74 us
    ppermute x3, starting transfers between devices, body(): query.append(lax.ppermute(query[0], 'rep', hops_out(hop, span_len)))  5.39 us
    ppermute x3, starting transfers between devices, body(): returned.append(lax.ppermute(parts[hop], 'rep', hops_back(hop, span_len)))  3.68 us
    ppermute x3, waiting for transfers between devices, body(): returned.append(lax.ppermute(parts[hop], 'rep', hops_back(hop, span_len)))  3.22 us
    ppermute x3, waiting for transfers between devices, body(): kv.append(lax.ppermute(packed, 'blk', hops_out(hop, spans)))  2.96 us
    pallas_call x3, Pallas kernels, body(): pl.pallas_call(lambda *refs, hop=hop: attend_kernel(hop, spans, *refs), o...  1.96 us
    pallas_call x1, Pallas kernels, body(): pl.pallas_call(lambda *refs: attend_fetch_kernel(spans, chunks, *refs), o...  1.89 us
    pallas_call x1, Pallas kernels, body(): pl.pallas_call(finish_kernel, out_shape=(shape, jax.ShapeDtypeStruct((hea...  1.19 us
  transfers between devices with their start and end apart: 11, of which 5 were waited for; matrix products, arithmetic and copies ran while one was open for 0% of the time, Pallas kernels for 18%

commit v1 on v0

--- a/solution.py
+++ b/solution.py
@@ -76,20 +76,34 @@
         copy.wait()
 
 
+def store_part(out_ref, kv_head, numer, top, total, factor):
+    tok = out_ref.shape[1]
+    heads = (out_ref.shape[0] - STAT_ROWS) // DH
+    some = total > 0.0
+    numer = (numer * jnp.where(some, 1.0 / total, 0.0)).astype(jnp.bfloat16)
+    log_sum = top * factor + jnp.where(some, jnp.log(total), 0.0)
+    high = log_sum.astype(jnp.bfloat16)
+    rest = log_sum - high.astype(jnp.float32)
+    middle = rest.astype(jnp.bfloat16)
+    low = (rest - middle.astype(jnp.float32)).astype(jnp.bfloat16)
+    for group in range(GROUP):
+        head = kv_head * GROUP + group
+        lanes = slice(group * tok, (group + 1) * tok)
+        out_ref[head * DH : (head + 1) * DH, :] = numer[:, lanes]
+        for at, stat in enumerate((high, middle, low)):
+            row = heads * DH + 3 * head + at
+            out_ref[row : row + 1, :] = stat[:, lanes]
+
+
 def attend_kernel(rep_hop, spans, bound_ref, query_ref, *refs):
     kv_refs, out_ref = refs[:spans], refs[spans]
     tok = bound_ref.shape[1]
     kv_heads = kv_refs[0].shape[0]
     factor = DH**-0.5
     lanes = GROUP * tok
-    ahead = lax.broadcasted_iota(jnp.int32, (tok, tok), 0) - lax.broadcasted_iota(
-        jnp.int32, (tok, tok), 1
-    )
-    ahead = jnp.concatenate([ahead] * GROUP, axis=1)
     for kv_head in range(kv_heads):
-        rows = slice(kv_head * lanes, (kv_head + 1) * lanes)
-        query = query_ref[rows, :]
-        scores = []
+        query = query_ref[kv_head * lanes : (kv_head + 1) * lanes, :]
+        scores, tops, allowed = [], [], []
         for hop in range(spans):
             raw = lax.dot_general(
                 kv_refs[hop][kv_head, 0],
@@ -99,15 +113,24 @@
             )
             at = rep_hop * spans + hop
             bound = jnp.concatenate([bound_ref[at : at + 1, :]] * GROUP, axis=1)
-            scores.append(jnp.where(ahead <= bound, raw, NEG_FILL))
-        top = scores[0]
+            if rep_hop == 0 and hop == 0:
+                ahead = lax.broadcasted_iota(jnp.int32, (tok, tok), 0) - lax.broadcasted_iota(
+                    jnp.int32, (tok, tok), 1
+                )
+                raw = jnp.where(jnp.concatenate([ahead] * GROUP, axis=1) <= 0, raw, NEG_FILL)
+            scores.append(raw)
+            allowed.append(bound >= 0)
+            tops.append(
+                jnp.where(bound >= 0, jnp.max(raw, axis=0, keepdims=True), NEG_FILL)
+            )
+        top = tops[0]
         for hop in range(1, spans):
-            top = jnp.maximum(top, scores[hop])
-        top = jnp.max(top, axis=0, keepdims=True)
-        weight_sum, numer = None, None
+            top = jnp.maximum(top, tops[hop])
+        total, numer = None, None
         for hop in range(spans):
-            weights = jnp.exp2((scores[hop] - top) * (factor * LOG2E))
-            weight_sum = weights if weight_sum is None else weight_sum + weights
+            chunk_top = jnp.where(allowed[hop], top, -NEG_FILL)
+            weights = jnp.exp2((scores[hop] - chunk_top) * (factor * LOG2E))
+            total = weights if total is None else total + weights
             term = lax.dot_general(
                 kv_refs[hop][kv_head, 1],
                 weights.astype(jnp.bfloat16),
@@ -115,16 +138,8 @@
                 preferred_element_type=jnp.float32,
             )
             numer = term if numer is None else numer + term
-        total = jnp.sum(weight_sum, axis=0, keepdims=True)
-        out_ref[0:DH, rows] = (numer * (1.0 / total)).astype(jnp.bfloat16)
-        log_sum = top * factor + jnp.log(total)
-        high = log_sum.astype(jnp.bfloat16)
-        rest = log_sum - high.astype(jnp.float32)
-        middle = rest.astype(jnp.bfloat16)
-        low = (rest - middle.astype(jnp.float32)).astype(jnp.bfloat16)
-        out_ref[DH : DH + STAT_ROWS, rows] = jnp.concatenate(
-            [high, middle, low, jnp.zeros((STAT_ROWS - 3, lanes), jnp.bfloat16)], axis=0
-        )
+        total = jnp.sum(total, axis=0, keepdims=True)
+        store_part(out_ref, kv_head, numer, top, total, factor)
 
 
 def attend_fetch_kernel(spans, chunks, *refs):
@@ -147,34 +162,35 @@
 
 def combine_kernel(*refs):
     part_refs, (attended_ref, log_sum_ref) = refs[:-2], refs[-2:]
-    stats = []
-    for part in part_refs:
-        parts = part[DH : DH + STAT_ROWS, :].astype(jnp.float32)
-        stats.append(parts[0:1] + parts[1:2] + parts[2:3])
-    top = stats[0]
-    for stat in stats[1:]:
-        top = jnp.maximum(top, stat)
-    shares = [jnp.exp(stat - top) for stat in stats]
-    total = shares[0]
-    for share in shares[1:]:
-        total = total + share
-    scale = 1.0 / total
-    numer = None
-    for part, share in zip(part_refs, shares):
-        term = part[0:DH, :].astype(jnp.float32) * (share * scale)
-        numer = term if numer is None else numer + term
-    attended_ref[...] = numer.astype(jnp.bfloat16)
-    log_sum = top + jnp.log(total)
-    tok = log_sum_ref.shape[1]
-    for head in range(log_sum_ref.shape[0]):
-        log_sum_ref[head : head + 1, :] = log_sum[:, head * tok : (head + 1) * tok]
-
-
-def project(attended_ref, weight_ref, tok, columns):
+    heads, _ = log_sum_ref.shape
+    for head in range(heads):
+        stats = []
+        for part in part_refs:
+            parts = part[heads * DH : heads * DH + STAT_ROWS, :].astype(jnp.float32)
+            row = 3 * head
+            stats.append(parts[row : row + 1] + parts[row + 1 : row + 2] + parts[row + 2 : row + 3])
+        top = stats[0]
+        for stat in stats[1:]:
+            top = jnp.maximum(top, stat)
+        shares = [jnp.exp(stat - top) for stat in stats]
+        total = shares[0]
+        for share in shares[1:]:
+            total = total + share
+        scale = 1.0 / total
+        rows = slice(head * DH, (head + 1) * DH)
+        numer = None
+        for part, share in zip(part_refs, shares):
+            term = part[rows, :].astype(jnp.float32) * (share * scale)
+            numer = term if numer is None else numer + term
+        attended_ref[rows, :] = numer.astype(jnp.bfloat16)
+        log_sum_ref[head : head + 1, :] = top + jnp.log(total)
+
+
+def project(attended_ref, weight_ref, columns):
     out = None
     for head in range(weight_ref.shape[0] // DH):
         term = lax.dot_general(
-            attended_ref[:, head * tok : (head + 1) * tok],
+            attended_ref[head * DH : (head + 1) * DH, :],
             weight_ref[head * DH : (head + 1) * DH, columns],
             (((0,), (0,)), ((), ())),
             preferred_element_type=jnp.float32,
@@ -184,13 +200,13 @@
 
 
 def project_home_kernel(attended_ref, weight_ref, out_ref):
-    out_ref[...] = project(attended_ref, weight_ref, out_ref.shape[0], slice(None))
+    out_ref[...] = project(attended_ref, weight_ref, slice(None))
 
 
 def finish_kernel(
     home_ref, other_ref, weight_ref, log_ref, out_hbm, log_hbm, out_ref, sems
 ):
-    tok, width = out_ref.shape
+    width = out_ref.shape[1]
     log_copy = pltpu.make_async_copy(log_ref, log_hbm, sems.at[0])
     log_copy.start()
     step = math.gcd(width, OUT_STEP)
@@ -199,7 +215,7 @@
     for at in range(width // step):
         here = slice(at * step, (at + 1) * step)
         columns = pl.ds(pl.multiple_of(base + at * step, 128), step)
-        other = project(other_ref, weight_ref, tok, columns)
+        other = project(other_ref, weight_ref, columns)
         out_ref[:, here] = (
             home_ref[:, here].astype(jnp.float32) + other.astype(jnp.float32)
         ).astype(jnp.bfloat16)
@@ -254,7 +270,7 @@
     for hop in range(1, span_len):
         query.append(lax.ppermute(query[0], "rep", hops_out(hop, span_len)))
     weight_away = lax.ppermute(out_weight, "head", [(0, 1), (1, 0)])
-    part_shape = jax.ShapeDtypeStruct((DH + STAT_ROWS, heads * tok), jnp.bfloat16)
+    part_shape = jax.ShapeDtypeStruct((heads * DH + STAT_ROWS, tok), jnp.bfloat16)
     attend = dict(
         cost_estimate=cost(
             4 * heads * tok * spans * tok * DH,
@@ -291,7 +307,7 @@
     attended, log_sum = pl.pallas_call(
         combine_kernel,
         out_shape=(
-            jax.ShapeDtypeStruct((DH, heads * tok), jnp.bfloat16),
+            jax.ShapeDtypeStruct((heads * DH, tok), jnp.bfloat16),
             jax.ShapeDtypeStruct((heads, tok), jnp.float32),
         ),
         in_specs=[VMEM] * span_len,

time: 30.9 us -> 30.9 us (level)
  no operation moved by 1% of the time
where the time goes in v1:
time: 30.9 us; the launch traced here: 30.6 us
  starting transfers between devices  16.4 us (53%)
  waiting for transfers between devices  6.9 us (22%)
  Pallas kernels  6.59 us (21%)
  between operations  0.71 us (2%)
    ppermute x3, starting transfers between devices, body(): kv.append(lax.ppermute(packed, 'blk', hops_out(hop, spans)))  6.74 us
    ppermute x3, starting transfers between devices, body(): query.append(lax.ppermute(query[0], 'rep', hops_out(hop, span_len)))  5.39 us
    ppermute x3, starting transfers between devices, body(): returned.append(lax.ppermute(parts[hop], 'rep', hops_back(hop, span_len)))  3.68 us
    ppermute x3, waiting for transfers between devices, body(): returned.append(lax.ppermute(parts[hop], 'rep', hops_back(hop, span_len)))  3.13 us
    ppermute x3, waiting for transfers between devices, body(): kv.append(lax.ppermute(packed, 'blk', hops_out(hop, spans)))  2.96 us
    pallas_call x3, Pallas kernels, body(): pl.pallas_call(lambda *refs, hop=hop: attend_kernel(hop, spans, *refs), o...  1.98 us
    pallas_call x1, Pallas kernels, body(): pl.pallas_call(lambda *refs: attend_fetch_kernel(spans, chunks, *refs), o...  1.9 us
    pallas_call x1, Pallas kernels, body(): pl.pallas_call(finish_kernel, out_shape=(shape, jax.ShapeDtypeStruct((hea...  1.19 us
  transfers between devices with their start and end apart: 11, of which 5 were waited for; matrix products, arithmetic and copies ran while one was open for 0% of the time, Pallas kernels for 18%

profile of v1, /device:TPU:0, one launch (start us, length us, event | category | flops | bytes accessed | tf_op | source)
XLA Modules:
  0.0 30.6 jit_solution(3112688635712665119)
XLA Ops:
  0.6 0.6 %collective-permute-start.10 = (bf16[384,3072]{1,0:T(8,128)(2,1)}, bf16[384,3072]{1,0:T(8,128)(2,1)S(1)}, u32[]{:S(2)}, u32[]{:S(2)}) collective-permute-start(bf16[384,3072]{1,0:T(8,128)(2,1)} %refs_6_.1), channel_id=1, source_target_pairs={{0,16},{16,0},{1,17},{17,1},{2,18},{18,2},{3,19},{19,3},{4,20},{20... | collective-permute-start | bytes 7077896 | tf_op jit(solution)/shard_map/ppermute | solution.py:272
  1.2 0.9 %pack.1 = (bf16[384,128]{1,0:T(8,128)(2,1)S(1)}, bf16[1,2,128,128]{3,2,1,0:T(8,128)(2,1)S(1)}, s32[16,128]{1,0:T(8,128)S(1)}) custom-call(bf16[128,384]{1,0:T(8,128)(2,1)} %refs_0_.1, bf16[128,128]{1,0:T(8,128)(2,1)} %refs_1_.1, bf16[128,128]{1,0:T(8,128)(2,1)} %refs_2_.1, s32[16]{0:T(128)} %refs_3_.1), custom_call_target="tpu_custom_call" | custom-call | tf_op jit(solution)/shard_map/pack/pallas_call | solution.py:250
  2.1 4.7 %collective-permute-start.2 = (bf16[1,2,128,128]{3,2,1,0:T(8,128)(2,1)S(1)}, bf16[1,2,128,128]{3,2,1,0:T(8,128)(2,1)S(1)}, u32[]{:S(2)}, u32[]{:S(2)}) collective-permute-start(bf16[1,2,128,128]{3,2,1,0:T(8,128)(2,1)S(1)} %get-tuple-element.11.refs_2_), channel_id=1, source_target_pairs={{0,12},{4,8},{8,4},{12,0},{1,13},{5,9},{9,5},{13,1},{2,14},{6,10},... | collective-permute-start | bytes 196616 | tf_op jit(solution)/shard_map/ppermute | solution.py:269
  6.8 0.0 collective-permute-start.1
  6.8 1.5 %collective-permute-start.3 = (bf16[384,128]{1,0:T(8,128)(2,1)S(1)}, bf16[384,128]{1,0:T(8,128)(2,1)S(1)}, u32[]{:S(2)}, u32[]{:S(2)}) collective-permute-start(bf16[384,128]{1,0:T(8,128)(2,1)S(1)} %get-tuple-element.10.refs_1_), channel_id=1, source_target_pairs={{0,1},{1,0},{2,3},{3,2},{4,5},{5,4},{6,7},{7,6},{8,9},{9,8},{10,11... | collective-permute-start | bytes 294920 | tf_op jit(solution)/shard_map/ppermute | solution.py:271
  8.3 1.5 %collective-permute-start.5 = (bf16[384,128]{1,0:T(8,128)(2,1)S(1)}, bf16[384,128]{1,0:T(8,128)(2,1)S(1)}, u32[]{:S(2)}, u32[]{:S(2)}) collective-permute-start(bf16[384,128]{1,0:T(8,128)(2,1)S(1)} %get-tuple-element.10.refs_1_), channel_id=1, source_target_pairs={{0,2},{1,3},{2,0},{3,1},{4,6},{5,7},{6,4},{7,5},{8,10},{9,11},{10,... | collective-permute-start | bytes 294920 | tf_op jit(solution)/shard_map/ppermute | solution.py:271
  9.8 2.4 %collective-permute-start.7 = (bf16[384,128]{1,0:T(8,128)(2,1)S(1)}, bf16[384,128]{1,0:T(8,128)(2,1)S(1)}, u32[]{:S(2)}, u32[]{:S(2)}) collective-permute-start(bf16[384,128]{1,0:T(8,128)(2,1)S(1)} %get-tuple-element.10.refs_1_), channel_id=1, source_target_pairs={{0,3},{1,2},{2,1},{3,0},{4,7},{5,6},{6,5},{7,4},{8,11},{9,10},{10,... | collective-permute-start | bytes 294920 | tf_op jit(solution)/shard_map/ppermute | solution.py:271
  12.2 0.7 %collective-permute-done.1.refs_4_ = bf16[1,2,128,128]{3,2,1,0:T(8,128)(2,1)S(1)} collective-permute-done((bf16[1,2,128,128]{3,2,1,0:T(8,128)(2,1)S(1)}, bf16[1,2,128,128]{3,2,1,0:T(8,128)(2,1)S(1)}, u32[]{:S(2)}, u32[]{:S(2)}) %collective-permute-start.1) | collective-permute-done | bytes 65568 | tf_op jit(solution)/shard_map/ppermute | solution.py:269
  12.9 2.1 %collective-permute-start = (bf16[1,2,128,128]{3,2,1,0:T(8,128)(2,1)S(1)}, bf16[1,2,128,128]{3,2,1,0:T(8,128)(2,1)S(1)}, u32[]{:S(2)}, u32[]{:S(2)}) collective-permute-start(bf16[1,2,128,128]{3,2,1,0:T(8,128)(2,1)S(1)} %get-tuple-element.11.refs_2_), channel_id=1, source_target_pairs={{0,4},{4,0},{8,12},{12,8},{1,5},{5,1},{9,13},{13,9},{2,6},{6,2},{1... | collective-permute-start | bytes 196616 | tf_op jit(solution)/shard_map/ppermute | solution.py:269
  15.0 2.2 %collective-permute-done.refs_3_ = bf16[1,2,128,128]{3,2,1,0:T(8,128)(2,1)S(1)} collective-permute-done((bf16[1,2,128,128]{3,2,1,0:T(8,128)(2,1)S(1)}, bf16[1,2,128,128]{3,2,1,0:T(8,128)(2,1)S(1)}, u32[]{:S(2)}, u32[]{:S(2)}) %collective-permute-start) | collective-permute-done | bytes 65568 | tf_op jit(solution)/shard_map/ppermute | solution.py:269
  17.2 0.7 %attend.3 = bf16[400,128]{1,0:T(8,128)(2,1)S(1)} custom-call(s32[16,128]{1,0:T(8,128)S(1)} %get-tuple-element.9.refs_0_, bf16[384,128]{1,0:T(8,128)(2,1)S(1)} %collective-permute-done.3.refs_1_, bf16[1,2,128,128]{3,2,1,0:T(8,128)(2,1)S(1)} %get-tuple-element.11.refs_2_, bf16[1,2,128,128]{3,2,1,0:T(8,128)(2,1)S(1)} %collective-permute-done.refs_3_, ...), custom_call_target="tpu_custom_call" | custom-call | flops 100663296 | bytes 458752 | tf_op jit(solution)/shard_map/attend/pallas_call | solution.py:286
  17.9 1.5 %collective-permute-start.4 = (bf16[400,128]{1,0:T(8,128)(2,1)S(1)}, bf16[400,128]{1,0:T(8,128)(2,1)S(1)}, u32[]{:S(2)}, u32[]{:S(2)}) collective-permute-start(bf16[400,128]{1,0:T(8,128)(2,1)S(1)} %attend.3), channel_id=1, source_target_pairs={{1,0},{0,1},{3,2},{2,3},{5,4},{4,5},{7,6},{6,7},{9,8},{8,9},{11,10... | collective-permute-start | bytes 307208 | tf_op jit(solution)/shard_map/ppermute | solution.py:306
  19.4 0.7 %attend.4 = bf16[400,128]{1,0:T(8,128)(2,1)S(1)} custom-call(s32[16,128]{1,0:T(8,128)S(1)} %get-tuple-element.9.refs_0_, bf16[384,128]{1,0:T(8,128)(2,1)S(1)} %collective-permute-done.5.refs_1_, bf16[1,2,128,128]{3,2,1,0:T(8,128)(2,1)S(1)} %get-tuple-element.11.refs_2_, bf16[1,2,128,128]{3,2,1,0:T(8,128)(2,1)S(1)} %collective-permute-done.refs_3_, ...), custom_call_target="tpu_custom_call" | custom-call | flops 100663296 | bytes 458752 | tf_op jit(solution)/shard_map/attend/pallas_call | solution.py:286
  20.1 1.6 %collective-permute-start.6 = (bf16[400,128]{1,0:T(8,128)(2,1)S(1)}, bf16[400,128]{1,0:T(8,128)(2,1)S(1)}, u32[]{:S(2)}, u32[]{:S(2)}) collective-permute-start(bf16[400,128]{1,0:T(8,128)(2,1)S(1)} %attend.4), channel_id=1, source_target_pairs={{2,0},{3,1},{0,2},{1,3},{6,4},{7,5},{4,6},{5,7},{10,8},{11,9},{8,1... | collective-permute-start | bytes 307208 | tf_op jit(solution)/shard_map/ppermute | solution.py:306
  21.7 0.7 %attend.5 = bf16[400,128]{1,0:T(8,128)(2,1)S(1)} custom-call(s32[16,128]{1,0:T(8,128)S(1)} %get-tuple-element.9.refs_0_, bf16[384,128]{1,0:T(8,128)(2,1)S(1)} %collective-permute-done.7.refs_1_, bf16[1,2,128,128]{3,2,1,0:T(8,128)(2,1)S(1)} %get-tuple-element.11.refs_2_, bf16[1,2,128,128]{3,2,1,0:T(8,128)(2,1)S(1)} %collective-permute-done.refs_3_, ...), custom_call_target="tpu_custom_call" | custom-call | flops 100663296 | bytes 458752 | tf_op jit(solution)/shard_map/attend/pallas_call | solution.py:286
  22.3 0.6 %collective-permute-start.8 = (bf16[400,128]{1,0:T(8,128)(2,1)S(1)}, bf16[400,128]{1,0:T(8,128)(2,1)S(1)}, u32[]{:S(2)}, u32[]{:S(2)}) collective-permute-start(bf16[400,128]{1,0:T(8,128)(2,1)S(1)} %attend.5), channel_id=1, source_target_pairs={{3,0},{2,1},{1,2},{0,3},{7,4},{6,5},{5,6},{4,7},{11,8},{10,9},{9,1... | collective-permute-start | bytes 307208 | tf_op jit(solution)/shard_map/ppermute | solution.py:306
  22.9 1.9 %attend_fetch.1 = (bf16[400,128]{1,0:T(8,128)(2,1)S(1)}, bf16[384,1536]{1,0:T(8,128)(2,1)S(1)}) custom-call(s32[16,128]{1,0:T(8,128)S(1)} %get-tuple-element.9.refs_0_, bf16[384,128]{1,0:T(8,128)(2,1)S(1)} %get-tuple-element.10.refs_1_, bf16[1,2,128,128]{3,2,1,0:T(8,128)(2,1)S(1)} %get-tuple-element.11.refs_2_, ...), custom_call_target="tpu_custom_call" | custom-call | flops 100663296 | bytes 458752 | tf_op jit(solution)/shard_map/attend_fetch/pallas_call | solution.py:295
  24.8 1.1 %collective-permute-done.6.refs_2_ = bf16[400,128]{1,0:T(8,128)(2,1)S(1)} collective-permute-done((bf16[400,128]{1,0:T(8,128)(2,1)S(1)}, bf16[400,128]{1,0:T(8,128)(2,1)S(1)}, u32[]{:S(2)}, u32[]{:S(2)}) %collective-permute-start.6) | collective-permute-done | bytes 102432 | tf_op jit(solution)/shard_map/ppermute | solution.py:306
  25.9 2.1 %collective-permute-done.8.refs_3_ = bf16[400,128]{1,0:T(8,128)(2,1)S(1)} collective-permute-done((bf16[400,128]{1,0:T(8,128)(2,1)S(1)}, bf16[400,128]{1,0:T(8,128)(2,1)S(1)}, u32[]{:S(2)}, u32[]{:S(2)}) %collective-permute-start.8) | collective-permute-done | bytes 102432 | tf_op jit(solution)/shard_map/ppermute | solution.py:306
  28.0 0.1 combine.1
  28.1 0.1 collective-permute-start.9
  28.2 0.5 %project_home.1.home_ref = bf16[128,1536]{1,0:T(8,128)(2,1)S(1)} custom-call(bf16[384,128]{1,0:T(8,128)(2,1)S(1)} %get-tuple-element.13.attended_ref, bf16[384,1536]{1,0:T(8,128)(2,1)S(1)} %get-tuple-element.14.weight_ref), custom_call_target="tpu_custom_call" | custom-call | flops 150994944 | bytes 1179648 | tf_op jit(solution)/shard_map/project_home/pallas_call | solution.py:320
  28.7 0.8 %collective-permute-done.9.other_ref = bf16[384,128]{1,0:T(8,128)(2,1)S(1)} collective-permute-done((bf16[384,128]{1,0:T(8,128)(2,1)S(1)}, bf16[384,128]{1,0:T(8,128)(2,1)S(1)}, u32[]{:S(2)}, u32[]{:S(2)}) %collective-permute-start.9) | collective-permute-done | bytes 98336 | tf_op jit(solution)/shard_map/ppermute | solution.py:318
  29.5 1.2 %finish.1 = (bf16[128,1536]{1,0:T(8,128)(2,1)}, f32[3,128]{1,0:T(4,128)}) custom-call(bf16[128,1536]{1,0:T(8,128)(2,1)S(1)} %project_home.1.home_ref, bf16[384,128]{1,0:T(8,128)(2,1)S(1)} %collective-permute-done.9.other_ref, bf16[384,3072]{1,0:T(8,128)(2,1)S(1)} %collective-permute-done.10.weight_ref, f32[3,128]{1,0:T(4,128)S(1)} %get-tuple-element.15.log_ref), custom_call_target="tpu_custom_call" | custom-call | tf_op jit(solution)/shard_map/finish/pallas_call | solution.py:329
  (6 shorter events, 0.0 us)
Async XLA Ops:
  0.6 28.8 %collective-permute-start.10 = (bf16[384,3072]{1,0:T(8,128)(2,1)}, bf16[384,3072]{1,0:T(8,128)(2,1)S(1)}, u32[]{:S(2)}, u32[]{:S(2)}) collective-permute-start(bf16[384,3072]{1,0:T(8,128)(2,1)} %refs_6_.1), channel_id=1, source_target_pairs={{0,16},{16,0},{1,17},{17,1},{2,18},{18,2},{3,19},{19,3},{4,20},{20... | collective-permute-start | bytes 7077896 | tf_op jit(solution)/shard_map/ppermute | solution.py:272
  2.1 7.7 %collective-permute-start.2 = (bf16[1,2,128,128]{3,2,1,0:T(8,128)(2,1)S(1)}, bf16[1,2,128,128]{3,2,1,0:T(8,128)(2,1)S(1)}, u32[]{:S(2)}, u32[]{:S(2)}) collective-permute-start(bf16[1,2,128,128]{3,2,1,0:T(8,128)(2,1)S(1)} %get-tuple-element.11.refs_2_), channel_id=1, source_target_pairs={{0,12},{4,8},{8,4},{12,0},{1,13},{5,9},{9,5},{13,1},{2,14},{6,10},... | collective-permute-start | bytes 196616 | tf_op jit(solution)/shard_map/ppermute | solution.py:269
  6.8 6.1 %collective-permute-start.1 = (bf16[1,2,128,128]{3,2,1,0:T(8,128)(2,1)S(1)}, bf16[1,2,128,128]{3,2,1,0:T(8,128)(2,1)S(1)}, u32[]{:S(2)}, u32[]{:S(2)}) collective-permute-start(bf16[1,2,128,128]{3,2,1,0:T(8,128)(2,1)S(1)} %get-tuple-element.11.refs_2_), channel_id=1, source_target_pairs={{0,8},{4,12},{8,0},{12,4},{1,9},{5,13},{9,1},{13,5},{2,10},{6,14},... | collective-permute-start | bytes 196616 | tf_op jit(solution)/shard_map/ppermute | solution.py:269
  6.8 10.4 %collective-permute-start.3 = (bf16[384,128]{1,0:T(8,128)(2,1)S(1)}, bf16[384,128]{1,0:T(8,128)(2,1)S(1)}, u32[]{:S(2)}, u32[]{:S(2)}) collective-permute-start(bf16[384,128]{1,0:T(8,128)(2,1)S(1)} %get-tuple-element.10.refs_1_), channel_id=1, source_target_pairs={{0,1},{1,0},{2,3},{3,2},{4,5},{5,4},{6,7},{7,6},{8,9},{9,8},{10,11... | collective-permute-start | bytes 294920 | tf_op jit(solution)/shard_map/ppermute | solution.py:271
  8.3 11.1 %collective-permute-start.5 = (bf16[384,128]{1,0:T(8,128)(2,1)S(1)}, bf16[384,128]{1,0:T(8,128)(2,1)S(1)}, u32[]{:S(2)}, u32[]{:S(2)}) collective-permute-start(bf16[384,128]{1,0:T(8,128)(2,1)S(1)} %get-tuple-element.10.refs_1_), channel_id=1, source_target_pairs={{0,2},{1,3},{2,0},{3,1},{4,6},{5,7},{6,4},{7,5},{8,10},{9,11},{10,... | collective-permute-start | bytes 294920 | tf_op jit(solution)/shard_map/ppermute | solution.py:271
  9.8 11.9 %collective-permute-start.7 = (bf16[384,128]{1,0:T(8,128)(2,1)S(1)}, bf16[384,128]{1,0:T(8,128)(2,1)S(1)}, u32[]{:S(2)}, u32[]{:S(2)}) collective-permute-start(bf16[384,128]{1,0:T(8,128)(2,1)S(1)} %get-tuple-element.10.refs_1_), channel_id=1, source_target_pairs={{0,3},{1,2},{2,1},{3,0},{4,7},{5,6},{6,5},{7,4},{8,11},{9,10},{10,... | collective-permute-start | bytes 294920 | tf_op jit(solution)/shard_map/ppermute | solution.py:271
  12.9 4.3 %collective-permute-start = (bf16[1,2,128,128]{3,2,1,0:T(8,128)(2,1)S(1)}, bf16[1,2,128,128]{3,2,1,0:T(8,128)(2,1)S(1)}, u32[]{:S(2)}, u32[]{:S(2)}) collective-permute-start(bf16[1,2,128,128]{3,2,1,0:T(8,128)(2,1)S(1)} %get-tuple-element.11.refs_2_), channel_id=1, source_target_pairs={{0,4},{4,0},{8,12},{12,8},{1,5},{5,1},{9,13},{13,9},{2,6},{6,2},{1... | collective-permute-start | bytes 196616 | tf_op jit(solution)/shard_map/ppermute | solution.py:269
  17.9 6.9 %collective-permute-start.4 = (bf16[400,128]{1,0:T(8,128)(2,1)S(1)}, bf16[400,128]{1,0:T(8,128)(2,1)S(1)}, u32[]{:S(2)}, u32[]{:S(2)}) collective-permute-start(bf16[400,128]{1,0:T(8,128)(2,1)S(1)} %attend.3), channel_id=1, source_target_pairs={{1,0},{0,1},{3,2},{2,3},{5,4},{4,5},{7,6},{6,7},{9,8},{8,9},{11,10... | collective-permute-start | bytes 307208 | tf_op jit(solution)/shard_map/ppermute | solution.py:306
  20.1 5.8 %collective-permute-start.6 = (bf16[400,128]{1,0:T(8,128)(2,1)S(1)}, bf16[400,128]{1,0:T(8,128)(2,1)S(1)}, u32[]{:S(2)}, u32[]{:S(2)}) collective-permute-start(bf16[400,128]{1,0:T(8,128)(2,1)S(1)} %attend.4), channel_id=1, source_target_pairs={{2,0},{3,1},{0,2},{1,3},{6,4},{7,5},{4,6},{5,7},{10,8},{11,9},{8,1... | collective-permute-start | bytes 307208 | tf_op jit(solution)/shard_map/ppermute | solution.py:306
  22.3 5.6 %collective-permute-start.8 = (bf16[400,128]{1,0:T(8,128)(2,1)S(1)}, bf16[400,128]{1,0:T(8,128)(2,1)S(1)}, u32[]{:S(2)}, u32[]{:S(2)}) collective-permute-start(bf16[400,128]{1,0:T(8,128)(2,1)S(1)} %attend.5), channel_id=1, source_target_pairs={{3,0},{2,1},{1,2},{0,3},{7,4},{6,5},{5,6},{4,7},{11,8},{10,9},{9,1... | collective-permute-start | bytes 307208 | tf_op jit(solution)/shard_map/ppermute | solution.py:306
  28.1 1.4 %collective-permute-start.9 = (bf16[384,128]{1,0:T(8,128)(2,1)S(1)}, bf16[384,128]{1,0:T(8,128)(2,1)S(1)}, u32[]{:S(2)}, u32[]{:S(2)}) collective-permute-start(bf16[384,128]{1,0:T(8,128)(2,1)S(1)} %get-tuple-element.13.attended_ref), channel_id=1, source_target_pairs={{0,16},{16,0},{1,17},{17,1},{2,18},{18,2},{3,19},{19,3},{4,20},{20... | collective-permute-start | bytes 294920 | tf_op jit(solution)/shard_map/ppermute | solution.py:318

commit v2 on v1

--- a/solution.py
+++ b/solution.py
@@ -103,37 +103,41 @@
     lanes = GROUP * tok
     for kv_head in range(kv_heads):
         query = query_ref[kv_head * lanes : (kv_head + 1) * lanes, :]
-        scores, tops, allowed = [], [], []
-        for hop in range(spans):
+        scores, allowed, top = [], [], None
+        for first in range(0, spans, 2):
+            pair = kv_refs[first : first + 2]
             raw = lax.dot_general(
-                kv_refs[hop][kv_head, 0],
+                jnp.concatenate([ref[kv_head, 0] for ref in pair], axis=0),
                 query,
                 (((1,), (1,)), ((), ())),
                 preferred_element_type=jnp.float32,
             )
-            at = rep_hop * spans + hop
-            bound = jnp.concatenate([bound_ref[at : at + 1, :]] * GROUP, axis=1)
-            if rep_hop == 0 and hop == 0:
-                ahead = lax.broadcasted_iota(jnp.int32, (tok, tok), 0) - lax.broadcasted_iota(
-                    jnp.int32, (tok, tok), 1
-                )
-                raw = jnp.where(jnp.concatenate([ahead] * GROUP, axis=1) <= 0, raw, NEG_FILL)
-            scores.append(raw)
-            allowed.append(bound >= 0)
-            tops.append(
-                jnp.where(bound >= 0, jnp.max(raw, axis=0, keepdims=True), NEG_FILL)
-            )
-        top = tops[0]
-        for hop in range(1, spans):
-            top = jnp.maximum(top, tops[hop])
+            for at in range(len(pair)):
+                hop = first + at
+                chunk = raw[at * tok : (at + 1) * tok, :]
+                if rep_hop == 0 and hop == 0:
+                    ahead = lax.broadcasted_iota(jnp.int32, (tok, tok), 0)
+                    ahead = ahead - lax.broadcasted_iota(jnp.int32, (tok, tok), 1)
+                    ahead = jnp.concatenate([ahead] * GROUP, axis=1)
+                    chunk = jnp.where(ahead <= 0, chunk, NEG_FILL)
+                row = rep_hop * spans + hop
+                bound = jnp.concatenate([bound_ref[row : row + 1, :]] * GROUP, axis=1)
+                scores.append(chunk)
+                allowed.append(bound >= 0)
+                chunk_top = jnp.max(chunk, axis=0, keepdims=True)
+                chunk_top = jnp.where(allowed[hop], chunk_top, NEG_FILL)
+                top = chunk_top if top is None else jnp.maximum(top, chunk_top)
         total, numer = None, None
-        for hop in range(spans):
-            chunk_top = jnp.where(allowed[hop], top, -NEG_FILL)
-            weights = jnp.exp2((scores[hop] - chunk_top) * (factor * LOG2E))
-            total = weights if total is None else total + weights
+        for first in range(0, spans, 2):
+            pair, weights = kv_refs[first : first + 2], []
+            for hop in range(first, first + len(pair)):
+                chunk_top = jnp.where(allowed[hop], top, -NEG_FILL)
+                weight = jnp.exp2((scores[hop] - chunk_top) * (factor * LOG2E))
+                total = weight if total is None else total + weight
+                weights.append(weight.astype(jnp.bfloat16))
             term = lax.dot_general(
-                kv_refs[hop][kv_head, 1],
-                weights.astype(jnp.bfloat16),
+                jnp.concatenate([ref[kv_head, 1] for ref in pair], axis=1),
+                jnp.concatenate(weights, axis=0),
                 (((1,), (0,)), ((), ())),
                 preferred_element_type=jnp.float32,
             )
@@ -187,16 +191,12 @@
 
 
 def project(attended_ref, weight_ref, columns):
-    out = None
-    for head in range(weight_ref.shape[0] // DH):
-        term = lax.dot_general(
-            attended_ref[head * DH : (head + 1) * DH, :],
-            weight_ref[head * DH : (head + 1) * DH, columns],
-            (((0,), (0,)), ((), ())),
-            preferred_element_type=jnp.float32,
-        )
-        out = term if out is None else out + term
-    return out.astype(jnp.bfloat16)
+    return lax.dot_general(
+        attended_ref[...],
+        weight_ref[:, columns],
+        (((0,), (0,)), ((), ())),
+        preferred_element_type=jnp.float32,
+    ).astype(jnp.bfloat16)
 
 
 def project_home_kernel(attended_ref, weight_ref, out_ref):

time: 30.9 us -> 30.7 us (level)
  transfers between devices with their start and end apart: 11 -> 11, of which waited for: 5 -> 5; matrix products, arithmetic and copies ran while one was open for 0% -> 0% of each run, Pallas kernels for 18% -> 17%
where the time goes in v2:
time: 30.7 us; the launch traced here: 30.5 us
  starting transfers between devices  16.4 us (53%)
  waiting for transfers between devices  7.03 us (23%)
  Pallas kernels  6.3 us (21%)
  between operations  0.71 us (2%)
    ppermute x3, starting transfers between devices, body(): kv.append(lax.ppermute(packed, 'blk', hops_out(hop, spans)))  6.74 us
    ppermute x3, starting transfers between devices, body(): query.append(lax.ppermute(query[0], 'rep', hops_out(hop, span_len)))  5.39 us
    ppermute x3, starting transfers between devices, body(): returned.append(lax.ppermute(parts[hop], 'rep', hops_back(hop, span_len)))  3.68 us
    ppermute x3, waiting for transfers between devices, body(): returned.append(lax.ppermute(parts[hop], 'rep', hops_back(hop, span_len)))  3.16 us
    ppermute x3, waiting for transfers between devices, body(): kv.append(lax.ppermute(packed, 'blk', hops_out(hop, spans)))  2.96 us
    pallas_call x3, Pallas kernels, body(): pl.pallas_call(lambda *refs, hop=hop: attend_kernel(hop, spans, *refs), o...  1.89 us
    pallas_call x1, Pallas kernels, body(): pl.pallas_call(lambda *refs: attend_fetch_kernel(spans, chunks, *refs), o...  1.87 us
    pallas_call x1, Pallas kernels, body(): pl.pallas_call(finish_kernel, out_shape=(shape, jax.ShapeDtypeStruct((hea...  1.11 us
  transfers between devices with their start and end apart: 11, of which 5 were waited for; matrix products, arithmetic and copies ran while one was open for 0% of the time, Pallas kernels for 17%

profile of v2, /device:TPU:0, one launch (start us, length us, event | category | flops | bytes accessed | tf_op | source)
XLA Modules:
  0.0 30.5 jit_solution(17074374634904979654)
XLA Ops:
  0.6 0.6 %collective-permute-start.10 = (bf16[384,3072]{1,0:T(8,128)(2,1)}, bf16[384,3072]{1,0:T(8,128)(2,1)S(1)}, u32[]{:S(2)}, u32[]{:S(2)}) collective-permute-start(bf16[384,3072]{1,0:T(8,128)(2,1)} %refs_6_.1), channel_id=1, source_target_pairs={{0,16},{16,0},{1,17},{17,1},{2,18},{18,2},{3,19},{19,3},{4,20},{20... | collective-permute-start | bytes 7077896 | tf_op jit(solution)/shard_map/ppermute | solution.py:272
  1.2 0.9 %pack.1 = (bf16[384,128]{1,0:T(8,128)(2,1)S(1)}, bf16[1,2,128,128]{3,2,1,0:T(8,128)(2,1)S(1)}, s32[16,128]{1,0:T(8,128)S(1)}) custom-call(bf16[128,384]{1,0:T(8,128)(2,1)} %refs_0_.1, bf16[128,128]{1,0:T(8,128)(2,1)} %refs_1_.1, bf16[128,128]{1,0:T(8,128)(2,1)} %refs_2_.1, s32[16]{0:T(128)} %refs_3_.1), custom_call_target="tpu_custom_call" | custom-call | tf_op jit(solution)/shard_map/pack/pallas_call | solution.py:250
  2.1 4.7 %collective-permute-start.2 = (bf16[1,2,128,128]{3,2,1,0:T(8,128)(2,1)S(1)}, bf16[1,2,128,128]{3,2,1,0:T(8,128)(2,1)S(1)}, u32[]{:S(2)}, u32[]{:S(2)}) collective-permute-start(bf16[1,2,128,128]{3,2,1,0:T(8,128)(2,1)S(1)} %get-tuple-element.11.refs_2_), channel_id=1, source_target_pairs={{0,12},{4,8},{8,4},{12,0},{1,13},{5,9},{9,5},{13,1},{2,14},{6,10},... | collective-permute-start | bytes 196616 | tf_op jit(solution)/shard_map/ppermute | solution.py:269
  6.8 0.0 collective-permute-start.1
  6.8 1.5 %collective-permute-start.3 = (bf16[384,128]{1,0:T(8,128)(2,1)S(1)}, bf16[384,128]{1,0:T(8,128)(2,1)S(1)}, u32[]{:S(2)}, u32[]{:S(2)}) collective-permute-start(bf16[384,128]{1,0:T(8,128)(2,1)S(1)} %get-tuple-element.10.refs_1_), channel_id=1, source_target_pairs={{0,1},{1,0},{2,3},{3,2},{4,5},{5,4},{6,7},{7,6},{8,9},{9,8},{10,11... | collective-permute-start | bytes 294920 | tf_op jit(solution)/shard_map/ppermute | solution.py:271
  8.3 1.5 %collective-permute-start.5 = (bf16[384,128]{1,0:T(8,128)(2,1)S(1)}, bf16[384,128]{1,0:T(8,128)(2,1)S(1)}, u32[]{:S(2)}, u32[]{:S(2)}) collective-permute-start(bf16[384,128]{1,0:T(8,128)(2,1)S(1)} %get-tuple-element.10.refs_1_), channel_id=1, source_target_pairs={{0,2},{1,3},{2,0},{3,1},{4,6},{5,7},{6,4},{7,5},{8,10},{9,11},{10,... | collective-permute-start | bytes 294920 | tf_op jit(solution)/shard_map/ppermute | solution.py:271
  9.8 2.4 %collective-permute-start.7 = (bf16[384,128]{1,0:T(8,128)(2,1)S(1)}, bf16[384,128]{1,0:T(8,128)(2,1)S(1)}, u32[]{:S(2)}, u32[]{:S(2)}) collective-permute-start(bf16[384,128]{1,0:T(8,128)(2,1)S(1)} %get-tuple-element.10.refs_1_), channel_id=1, source_target_pairs={{0,3},{1,2},{2,1},{3,0},{4,7},{5,6},{6,5},{7,4},{8,11},{9,10},{10,... | collective-permute-start | bytes 294920 | tf_op jit(solution)/shard_map/ppermute | solution.py:271
  12.2 0.7 %collective-permute-done.1.refs_4_ = bf16[1,2,128,128]{3,2,1,0:T(8,128)(2,1)S(1)} collective-permute-done((bf16[1,2,128,128]{3,2,1,0:T(8,128)(2,1)S(1)}, bf16[1,2,128,128]{3,2,1,0:T(8,128)(2,1)S(1)}, u32[]{:S(2)}, u32[]{:S(2)}) %collective-permute-start.1) | collective-permute-done | bytes 65568 | tf_op jit(solution)/shard_map/ppermute | solution.py:269
  12.9 2.1 %collective-permute-start = (bf16[1,2,128,128]{3,2,1,0:T(8,128)(2,1)S(1)}, bf16[1,2,128,128]{3,2,1,0:T(8,128)(2,1)S(1)}, u32[]{:S(2)}, u32[]{:S(2)}) collective-permute-start(bf16[1,2,128,128]{3,2,1,0:T(8,128)(2,1)S(1)} %get-tuple-element.11.refs_2_), channel_id=1, source_target_pairs={{0,4},{4,0},{8,12},{12,8},{1,5},{5,1},{9,13},{13,9},{2,6},{6,2},{1... | collective-permute-start | bytes 196616 | tf_op jit(solution)/shard_map/ppermute | solution.py:269
  15.0 2.2 %collective-permute-done.refs_3_ = bf16[1,2,128,128]{3,2,1,0:T(8,128)(2,1)S(1)} collective-permute-done((bf16[1,2,128,128]{3,2,1,0:T(8,128)(2,1)S(1)}, bf16[1,2,128,128]{3,2,1,0:T(8,128)(2,1)S(1)}, u32[]{:S(2)}, u32[]{:S(2)}) %collective-permute-start) | collective-permute-done | bytes 65568 | tf_op jit(solution)/shard_map/ppermute | solution.py:269
  17.2 0.6 %attend.3 = bf16[400,128]{1,0:T(8,128)(2,1)S(1)} custom-call(s32[16,128]{1,0:T(8,128)S(1)} %get-tuple-element.9.refs_0_, bf16[384,128]{1,0:T(8,128)(2,1)S(1)} %collective-permute-done.3.refs_1_, bf16[1,2,128,128]{3,2,1,0:T(8,128)(2,1)S(1)} %get-tuple-element.11.refs_2_, bf16[1,2,128,128]{3,2,1,0:T(8,128)(2,1)S(1)} %collective-permute-done.refs_3_, ...), custom_call_target="tpu_custom_call" | custom-call | flops 100663296 | bytes 458752 | tf_op jit(solution)/shard_map/attend/pallas_call | solution.py:286
  17.9 1.5 %collective-permute-start.4 = (bf16[400,128]{1,0:T(8,128)(2,1)S(1)}, bf16[400,128]{1,0:T(8,128)(2,1)S(1)}, u32[]{:S(2)}, u32[]{:S(2)}) collective-permute-start(bf16[400,128]{1,0:T(8,128)(2,1)S(1)} %attend.3), channel_id=1, source_target_pairs={{1,0},{0,1},{3,2},{2,3},{5,4},{4,5},{7,6},{6,7},{9,8},{8,9},{11,10... | collective-permute-start | bytes 307208 | tf_op jit(solution)/shard_map/ppermute | solution.py:306
  19.4 0.6 %attend.4 = bf16[400,128]{1,0:T(8,128)(2,1)S(1)} custom-call(s32[16,128]{1,0:T(8,128)S(1)} %get-tuple-element.9.refs_0_, bf16[384,128]{1,0:T(8,128)(2,1)S(1)} %collective-permute-done.5.refs_1_, bf16[1,2,128,128]{3,2,1,0:T(8,128)(2,1)S(1)} %get-tuple-element.11.refs_2_, bf16[1,2,128,128]{3,2,1,0:T(8,128)(2,1)S(1)} %collective-permute-done.refs_3_, ...), custom_call_target="tpu_custom_call" | custom-call | flops 100663296 | bytes 458752 | tf_op jit(solution)/shard_map/attend/pallas_call | solution.py:286
  20.0 1.6 %collective-permute-start.6 = (bf16[400,128]{1,0:T(8,128)(2,1)S(1)}, bf16[400,128]{1,0:T(8,128)(2,1)S(1)}, u32[]{:S(2)}, u32[]{:S(2)}) collective-permute-start(bf16[400,128]{1,0:T(8,128)(2,1)S(1)} %attend.4), channel_id=1, source_target_pairs={{2,0},{3,1},{0,2},{1,3},{6,4},{7,5},{4,6},{5,7},{10,8},{11,9},{8,1... | collective-permute-start | bytes 307208 | tf_op jit(solution)/shard_map/ppermute | solution.py:306
  21.6 0.6 %attend.5 = bf16[400,128]{1,0:T(8,128)(2,1)S(1)} custom-call(s32[16,128]{1,0:T(8,128)S(1)} %get-tuple-element.9.refs_0_, bf16[384,128]{1,0:T(8,128)(2,1)S(1)} %collective-permute-done.7.refs_1_, bf16[1,2,128,128]{3,2,1,0:T(8,128)(2,1)S(1)} %get-tuple-element.11.refs_2_, bf16[1,2,128,128]{3,2,1,0:T(8,128)(2,1)S(1)} %collective-permute-done.refs_3_, ...), custom_call_target="tpu_custom_call" | custom-call | flops 100663296 | bytes 458752 | tf_op jit(solution)/shard_map/attend/pallas_call | solution.py:286
  22.2 0.6 %collective-permute-start.8 = (bf16[400,128]{1,0:T(8,128)(2,1)S(1)}, bf16[400,128]{1,0:T(8,128)(2,1)S(1)}, u32[]{:S(2)}, u32[]{:S(2)}) collective-permute-start(bf16[400,128]{1,0:T(8,128)(2,1)S(1)} %attend.5), channel_id=1, source_target_pairs={{3,0},{2,1},{1,2},{0,3},{7,4},{6,5},{5,6},{4,7},{11,8},{10,9},{9,1... | collective-permute-start | bytes 307208 | tf_op jit(solution)/shard_map/ppermute | solution.py:306
  22.8 1.9 %attend_fetch.1 = (bf16[400,128]{1,0:T(8,128)(2,1)S(1)}, bf16[384,1536]{1,0:T(8,128)(2,1)S(1)}) custom-call(s32[16,128]{1,0:T(8,128)S(1)} %get-tuple-element.9.refs_0_, bf16[384,128]{1,0:T(8,128)(2,1)S(1)} %get-tuple-element.10.refs_1_, bf16[1,2,128,128]{3,2,1,0:T(8,128)(2,1)S(1)} %get-tuple-element.11.refs_2_, ...), custom_call_target="tpu_custom_call" | custom-call | flops 100663296 | bytes 458752 | tf_op jit(solution)/shard_map/attend_fetch/pallas_call | solution.py:295
  24.7 1.1 %collective-permute-done.6.refs_2_ = bf16[400,128]{1,0:T(8,128)(2,1)S(1)} collective-permute-done((bf16[400,128]{1,0:T(8,128)(2,1)S(1)}, bf16[400,128]{1,0:T(8,128)(2,1)S(1)}, u32[]{:S(2)}, u32[]{:S(2)}) %collective-permute-start.6) | collective-permute-done | bytes 102432 | tf_op jit(solution)/shard_map/ppermute | solution.py:306
  25.8 2.0 %collective-permute-done.8.refs_3_ = bf16[400,128]{1,0:T(8,128)(2,1)S(1)} collective-permute-done((bf16[400,128]{1,0:T(8,128)(2,1)S(1)}, bf16[400,128]{1,0:T(8,128)(2,1)S(1)}, u32[]{:S(2)}, u32[]{:S(2)}) %collective-permute-start.8) | collective-permute-done | bytes 102432 | tf_op jit(solution)/shard_map/ppermute | solution.py:306
  27.9 0.1 combine.1
  28.0 0.1 collective-permute-start.9
  28.1 0.4 %project_home.1.home_ref = bf16[128,1536]{1,0:T(8,128)(2,1)S(1)} custom-call(bf16[384,128]{1,0:T(8,128)(2,1)S(1)} %get-tuple-element.13.attended_ref, bf16[384,1536]{1,0:T(8,128)(2,1)S(1)} %get-tuple-element.14.weight_ref), custom_call_target="tpu_custom_call" | custom-call | flops 150994944 | bytes 1179648 | tf_op jit(solution)/shard_map/project_home/pallas_call | solution.py:320
  28.5 0.9 %collective-permute-done.9.other_ref = bf16[384,128]{1,0:T(8,128)(2,1)S(1)} collective-permute-done((bf16[384,128]{1,0:T(8,128)(2,1)S(1)}, bf16[384,128]{1,0:T(8,128)(2,1)S(1)}, u32[]{:S(2)}, u32[]{:S(2)}) %collective-permute-start.9) | collective-permute-done | bytes 98336 | tf_op jit(solution)/shard_map/ppermute | solution.py:318
  29.4 1.1 %finish.1 = (bf16[128,1536]{1,0:T(8,128)(2,1)}, f32[3,128]{1,0:T(4,128)}) custom-call(bf16[128,1536]{1,0:T(8,128)(2,1)S(1)} %project_home.1.home_ref, bf16[384,128]{1,0:T(8,128)(2,1)S(1)} %collective-permute-done.9.other_ref, bf16[384,3072]{1,0:T(8,128)(2,1)S(1)} %collective-permute-done.10.weight_ref, f32[3,128]{1,0:T(4,128)S(1)} %get-tuple-element.15.log_ref), custom_call_target="tpu_custom_call" | custom-call | tf_op jit(solution)/shard_map/finish/pallas_call | solution.py:329
  (6 shorter events, 0.0 us)
Async XLA Ops:
  0.6 28.7 %collective-permute-start.10 = (bf16[384,3072]{1,0:T(8,128)(2,1)}, bf16[384,3072]{1,0:T(8,128)(2,1)S(1)}, u32[]{:S(2)}, u32[]{:S(2)}) collective-permute-start(bf16[384,3072]{1,0:T(8,128)(2,1)} %refs_6_.1), channel_id=1, source_target_pairs={{0,16},{16,0},{1,17},{17,1},{2,18},{18,2},{3,19},{19,3},{4,20},{20... | collective-permute-start | bytes 7077896 | tf_op jit(solution)/shard_map/ppermute | solution.py:272
  2.1 7.7 %collective-permute-start.2 = (bf16[1,2,128,128]{3,2,1,0:T(8,128)(2,1)S(1)}, bf16[1,2,128,128]{3,2,1,0:T(8,128)(2,1)S(1)}, u32[]{:S(2)}, u32[]{:S(2)}) collective-permute-start(bf16[1,2,128,128]{3,2,1,0:T(8,128)(2,1)S(1)} %get-tuple-element.11.refs_2_), channel_id=1, source_target_pairs={{0,12},{4,8},{8,4},{12,0},{1,13},{5,9},{9,5},{13,1},{2,14},{6,10},... | collective-permute-start | bytes 196616 | tf_op jit(solution)/shard_map/ppermute | solution.py:269
  6.8 6.1 %collective-permute-start.1 = (bf16[1,2,128,128]{3,2,1,0:T(8,128)(2,1)S(1)}, bf16[1,2,128,128]{3,2,1,0:T(8,128)(2,1)S(1)}, u32[]{:S(2)}, u32[]{:S(2)}) collective-permute-start(bf16[1,2,128,128]{3,2,1,0:T(8,128)(2,1)S(1)} %get-tuple-element.11.refs_2_), channel_id=1, source_target_pairs={{0,8},{4,12},{8,0},{12,4},{1,9},{5,13},{9,1},{13,5},{2,10},{6,14},... | collective-permute-start | bytes 196616 | tf_op jit(solution)/shard_map/ppermute | solution.py:269
  6.8 10.4 %collective-permute-start.3 = (bf16[384,128]{1,0:T(8,128)(2,1)S(1)}, bf16[384,128]{1,0:T(8,128)(2,1)S(1)}, u32[]{:S(2)}, u32[]{:S(2)}) collective-permute-start(bf16[384,128]{1,0:T(8,128)(2,1)S(1)} %get-tuple-element.10.refs_1_), channel_id=1, source_target_pairs={{0,1},{1,0},{2,3},{3,2},{4,5},{5,4},{6,7},{7,6},{8,9},{9,8},{10,11... | collective-permute-start | bytes 294920 | tf_op jit(solution)/shard_map/ppermute | solution.py:271
  8.3 11.1 %collective-permute-start.5 = (bf16[384,128]{1,0:T(8,128)(2,1)S(1)}, bf16[384,128]{1,0:T(8,128)(2,1)S(1)}, u32[]{:S(2)}, u32[]{:S(2)}) collective-permute-start(bf16[384,128]{1,0:T(8,128)(2,1)S(1)} %get-tuple-element.10.refs_1_), channel_id=1, source_target_pairs={{0,2},{1,3},{2,0},{3,1},{4,6},{5,7},{6,4},{7,5},{8,10},{9,11},{10,... | collective-permute-start | bytes 294920 | tf_op jit(solution)/shard_map/ppermute | solution.py:271
  9.8 11.8 %collective-permute-start.7 = (bf16[384,128]{1,0:T(8,128)(2,1)S(1)}, bf16[384,128]{1,0:T(8,128)(2,1)S(1)}, u32[]{:S(2)}, u32[]{:S(2)}) collective-permute-start(bf16[384,128]{1,0:T(8,128)(2,1)S(1)} %get-tuple-element.10.refs_1_), channel_id=1, source_target_pairs={{0,3},{1,2},{2,1},{3,0},{4,7},{5,6},{6,5},{7,4},{8,11},{9,10},{10,... | collective-permute-start | bytes 294920 | tf_op jit(solution)/shard_map/ppermute | solution.py:271
  12.9 4.3 %collective-permute-start = (bf16[1,2,128,128]{3,2,1,0:T(8,128)(2,1)S(1)}, bf16[1,2,128,128]{3,2,1,0:T(8,128)(2,1)S(1)}, u32[]{:S(2)}, u32[]{:S(2)}) collective-permute-start(bf16[1,2,128,128]{3,2,1,0:T(8,128)(2,1)S(1)} %get-tuple-element.11.refs_2_), channel_id=1, source_target_pairs={{0,4},{4,0},{8,12},{12,8},{1,5},{5,1},{9,13},{13,9},{2,6},{6,2},{1... | collective-permute-start | bytes 196616 | tf_op jit(solution)/shard_map/ppermute | solution.py:269
  17.9 6.8 %collective-permute-start.4 = (bf16[400,128]{1,0:T(8,128)(2,1)S(1)}, bf16[400,128]{1,0:T(8,128)(2,1)S(1)}, u32[]{:S(2)}, u32[]{:S(2)}) collective-permute-start(bf16[400,128]{1,0:T(8,128)(2,1)S(1)} %attend.3), channel_id=1, source_target_pairs={{1,0},{0,1},{3,2},{2,3},{5,4},{4,5},{7,6},{6,7},{9,8},{8,9},{11,10... | collective-permute-start | bytes 307208 | tf_op jit(solution)/shard_map/ppermute | solution.py:306
  20.0 5.8 %collective-permute-start.6 = (bf16[400,128]{1,0:T(8,128)(2,1)S(1)}, bf16[400,128]{1,0:T(8,128)(2,1)S(1)}, u32[]{:S(2)}, u32[]{:S(2)}) collective-permute-start(bf16[400,128]{1,0:T(8,128)(2,1)S(1)} %attend.4), channel_id=1, source_target_pairs={{2,0},{3,1},{0,2},{1,3},{6,4},{7,5},{4,6},{5,7},{10,8},{11,9},{8,1... | collective-permute-start | bytes 307208 | tf_op jit(solution)/shard_map/ppermute | solution.py:306
  22.2 5.6 %collective-permute-start.8 = (bf16[400,128]{1,0:T(8,128)(2,1)S(1)}, bf16[400,128]{1,0:T(8,128)(2,1)S(1)}, u32[]{:S(2)}, u32[]{:S(2)}) collective-permute-start(bf16[400,128]{1,0:T(8,128)(2,1)S(1)} %attend.5), channel_id=1, source_target_pairs={{3,0},{2,1},{1,2},{0,3},{7,4},{6,5},{5,6},{4,7},{11,8},{10,9},{9,1... | collective-permute-start | bytes 307208 | tf_op jit(solution)/shard_map/ppermute | solution.py:306
  28.0 1.4 %collective-permute-start.9 = (bf16[384,128]{1,0:T(8,128)(2,1)S(1)}, bf16[384,128]{1,0:T(8,128)(2,1)S(1)}, u32[]{:S(2)}, u32[]{:S(2)}) collective-permute-start(bf16[384,128]{1,0:T(8,128)(2,1)S(1)} %get-tuple-element.13.attended_ref), channel_id=1, source_target_pairs={{0,16},{16,0},{1,17},{17,1},{2,18},{18,2},{3,19},{19,3},{4,20},{20... | collective-permute-start | bytes 294920 | tf_op jit(solution)/shard_map/ppermute | solution.py:318

commit v3 on v2

--- a/solution.py
+++ b/solution.py
@@ -38,30 +38,27 @@
 
 def pack_kernel(
     spans, span_len, query_hbm, keys_hbm, values_hbm, order_hbm,
-    query_ref, packed_ref, bound_ref, values_ref, order_ref, sems,
+    query_ref, packed_ref, bound_ref, order_ref, sems,
 ):
-    tok = values_ref.shape[0]
-    heads, kv_heads = query_ref.shape[0] // tok, packed_ref.shape[0]
+    kv_heads, _, tok, _ = packed_ref.shape
+    heads = query_ref.shape[0] // tok
     order_copy = pltpu.make_async_copy(order_hbm, order_ref, sems.at[0])
-    value_copy = pltpu.make_async_copy(values_hbm, values_ref, sems.at[1])
     copies = []
     for head in range(kv_heads):
-        copies.append((keys_hbm.at[:, pl.ds(head * DH, DH)], packed_ref.at[head, 0]))
+        columns = pl.ds(head * DH, DH)
+        copies.append((keys_hbm.at[:, columns], packed_ref.at[head, 0]))
+        copies.append((values_hbm.at[:, columns], packed_ref.at[head, 1]))
     for head in range(heads):
         copies.append(
             (query_hbm.at[:, pl.ds(head * DH, DH)], query_ref.at[pl.ds(head * tok, tok), :])
         )
     copies = [
-        pltpu.make_async_copy(source, target, sems.at[2 + at])
+        pltpu.make_async_copy(source, target, sems.at[1 + at])
         for at, (source, target) in enumerate(copies)
     ]
-    value_copy.start()
     order_copy.start()
     for copy in copies:
         copy.start()
-    value_copy.wait()
-    for head in range(kv_heads):
-        packed_ref[head, 1] = values_ref[:, head * DH : (head + 1) * DH].T
     order_copy.wait()
     blk_rank, rep_rank = lax.axis_index("blk"), lax.axis_index("rep")
     for rep_hop in range(span_len):
@@ -74,6 +71,16 @@
             )
     for copy in copies:
         copy.wait()
+
+
+def prepare_kernel(*refs):
+    kv_refs, (keys_ref, values_ref) = refs[:-2], refs[-2:]
+    for at, ref in enumerate(kv_refs):
+        kv_heads, _, tok, _ = ref.shape
+        here = slice(at * tok, (at + 1) * tok)
+        for kv_head in range(kv_heads):
+            keys_ref[kv_head, here, :] = ref[kv_head, 0]
+            values_ref[kv_head, :, here] = ref[kv_head, 1].T
 
 
 def store_part(out_ref, kv_head, numer, top, total, factor):
@@ -95,24 +102,23 @@
             out_ref[row : row + 1, :] = stat[:, lanes]
 
 
-def attend_kernel(rep_hop, spans, bound_ref, query_ref, *refs):
-    kv_refs, out_ref = refs[:spans], refs[spans]
+def attend_kernel(rep_hop, spans, bound_ref, query_ref, keys_ref, values_ref, out_ref):
     tok = bound_ref.shape[1]
-    kv_heads = kv_refs[0].shape[0]
+    kv_heads = keys_ref.shape[0]
     factor = DH**-0.5
     lanes = GROUP * tok
     for kv_head in range(kv_heads):
         query = query_ref[kv_head * lanes : (kv_head + 1) * lanes, :]
         scores, allowed, top = [], [], None
         for first in range(0, spans, 2):
-            pair = kv_refs[first : first + 2]
+            count = min(2, spans - first)
             raw = lax.dot_general(
-                jnp.concatenate([ref[kv_head, 0] for ref in pair], axis=0),
+                keys_ref[kv_head, first * tok : (first + count) * tok, :],
                 query,
                 (((1,), (1,)), ((), ())),
                 preferred_element_type=jnp.float32,
             )
-            for at in range(len(pair)):
+            for at in range(count):
                 hop = first + at
                 chunk = raw[at * tok : (at + 1) * tok, :]
                 if rep_hop == 0 and hop == 0:
@@ -129,14 +135,14 @@
                 top = chunk_top if top is None else jnp.maximum(top, chunk_top)
         total, numer = None, None
         for first in range(0, spans, 2):
-            pair, weights = kv_refs[first : first + 2], []
-            for hop in range(first, first + len(pair)):
+            count, weights = min(2, spans - first), []
+            for hop in range(first, first + count):
                 chunk_top = jnp.where(allowed[hop], top, -NEG_FILL)
                 weight = jnp.exp2((scores[hop] - chunk_top) * (factor * LOG2E))
                 total = weight if total is None else total + weight
                 weights.append(weight.astype(jnp.bfloat16))
             term = lax.dot_general(
-                jnp.concatenate([ref[kv_head, 1] for ref in pair], axis=1),
+                values_ref[kv_head, :, first * tok : (first + count) * tok],
                 jnp.concatenate(weights, axis=0),
                 (((1,), (0,)), ((), ())),
                 preferred_element_type=jnp.float32,
@@ -257,9 +263,8 @@
         in_specs=[HBM] * 4,
         out_specs=(VMEM, VMEM, VMEM),
         scratch_shapes=[
-            pltpu.VMEM((tok, kv_heads * DH), jnp.bfloat16),
             pltpu.SMEM(stretch_order.shape, jnp.int32),
-            pltpu.SemaphoreType.DMA((2 + kv_heads + heads,)),
+            pltpu.SemaphoreType.DMA((1 + 2 * kv_heads + heads,)),
         ],
         compiler_params=params(4),
         name="pack",
@@ -270,6 +275,17 @@
     for hop in range(1, span_len):
         query.append(lax.ppermute(query[0], "rep", hops_out(hop, span_len)))
     weight_away = lax.ppermute(out_weight, "head", [(0, 1), (1, 0)])
+    keys_all, values_all = pl.pallas_call(
+        prepare_kernel,
+        out_shape=(
+            jax.ShapeDtypeStruct((kv_heads, spans * tok, DH), jnp.bfloat16),
+            jax.ShapeDtypeStruct((kv_heads, DH, spans * tok), jnp.bfloat16),
+        ),
+        in_specs=[VMEM] * spans,
+        out_specs=(VMEM, VMEM),
+        compiler_params=params(8),
+        name="prepare",
+    )(*kv)
     part_shape = jax.ShapeDtypeStruct((heads * DH + STAT_ROWS, tok), jnp.bfloat16)
     attend = dict(
         cost_estimate=cost(
@@ -286,21 +302,21 @@
             pl.pallas_call(
                 lambda *refs, hop=hop: attend_kernel(hop, spans, *refs),
                 out_shape=part_shape,
-                in_specs=[VMEM] * (2 + spans),
+                in_specs=[VMEM] * 4,
                 out_specs=VMEM,
                 name="attend",
                 **attend,
-            )(bounds, query[hop], *kv)
+            )(bounds, query[hop], keys_all, values_all)
         )
     parts[0], weight = pl.pallas_call(
         lambda *refs: attend_fetch_kernel(spans, chunks, *refs),
         out_shape=(part_shape, jax.ShapeDtypeStruct((heads * DH, width), jnp.bfloat16)),
-        in_specs=[VMEM] * (2 + spans) + [HBM],
+        in_specs=[VMEM] * 4 + [HBM],
         out_specs=(VMEM, VMEM),
         scratch_shapes=[pltpu.SemaphoreType.DMA((chunks,))],
         name="attend_fetch",
         **attend,
-    )(bounds, query[0], *kv, in_hbm(out_weight))
+    )(bounds, query[0], keys_all, values_all, in_hbm(out_weight))
     returned = [parts[0]]
     for hop in range(1, span_len):
         returned.append(lax.ppermute(parts[hop], "rep", hops_back(hop, span_len)))

time: 30.7 us -> 30.7 us (level)
  no operation moved by 1% of the time
where the time goes in v3:
time: 30.7 us; the launch traced here: 30.5 us
  starting transfers between devices  16.4 us (53%)
  waiting for transfers between devices  7.01 us (23%)
  Pallas kernels  6.33 us (21%)
  between operations  0.73 us (2%)
    ppermute x3, starting transfers between devices, body(): kv.append(lax.ppermute(packed, 'blk', hops_out(hop, spans)))  6.74 us
    ppermute x3, starting transfers between devices, body(): query.append(lax.ppermute(query[0], 'rep', hops_out(hop, span_len)))  5.39 us
    ppermute x3, starting transfers between devices, body(): returned.append(lax.ppermute(parts[hop], 'rep', hops_back(hop, span_len)))  3.68 us
    ppermute x3, waiting for transfers between devices, body(): returned.append(lax.ppermute(parts[hop], 'rep', hops_back(hop, span_len)))  3.16 us
    ppermute x3, waiting for transfers between devices, body(): kv.append(lax.ppermute(packed, 'blk', hops_out(hop, spans)))  2.96 us
    pallas_call x3, Pallas kernels, body(): pl.pallas_call(lambda *refs, hop=hop: attend_kernel(hop, spans, *refs), o...  1.89 us
    pallas_call x1, Pallas kernels, body(): pl.pallas_call(lambda *refs: attend_fetch_kernel(spans, chunks, *refs), o...  1.87 us
    pallas_call x1, Pallas kernels, body(): pl.pallas_call(finish_kernel, out_shape=(shape, jax.ShapeDtypeStruct((hea...  1.09 us
  transfers between devices with their start and end apart: 11, of which 5 were waited for; matrix products, arithmetic and copies ran while one was open for 0% of the time, Pallas kernels for 17%

profile of v3, /device:TPU:0, one launch (start us, length us, event | category | flops | bytes accessed | tf_op | source)
XLA Modules:
  0.0 30.5 jit_solution(16801031410427066291)
XLA Ops:
  0.6 0.6 %collective-permute-start.10 = (bf16[384,3072]{1,0:T(8,128)(2,1)}, bf16[384,3072]{1,0:T(8,128)(2,1)S(1)}, u32[]{:S(2)}, u32[]{:S(2)}) collective-permute-start(bf16[384,3072]{1,0:T(8,128)(2,1)} %refs_4_.1), channel_id=1, source_target_pairs={{0,16},{16,0},{1,17},{17,1},{2,18},{18,2},{3,19},{19,3},{4,20},{20... | collective-permute-start | bytes 7077896 | tf_op jit(solution)/shard_map/ppermute | solution.py:277
  1.2 0.9 %pack.1 = (bf16[384,128]{1,0:T(8,128)(2,1)S(1)}, bf16[1,2,128,128]{3,2,1,0:T(8,128)(2,1)S(1)}, s32[16,128]{1,0:T(8,128)S(1)}) custom-call(bf16[128,384]{1,0:T(8,128)(2,1)} %refs_0_.1, bf16[128,128]{1,0:T(8,128)(2,1)} %refs_1_.1, bf16[128,128]{1,0:T(8,128)(2,1)} %refs_2_.1, s32[16]{0:T(128)} %refs_3_.1), custom_call_target="tpu_custom_call" | custom-call | tf_op jit(solution)/shard_map/pack/pallas_call | solution.py:256
  2.1 4.7 %collective-permute-start.2 = (bf16[1,2,128,128]{3,2,1,0:T(8,128)(2,1)S(1)}, bf16[1,2,128,128]{3,2,1,0:T(8,128)(2,1)S(1)}, u32[]{:S(2)}, u32[]{:S(2)}) collective-permute-start(bf16[1,2,128,128]{3,2,1,0:T(8,128)(2,1)S(1)} %get-tuple-element.13.refs_0_), channel_id=1, source_target_pairs={{0,12},{4,8},{8,4},{12,0},{1,13},{5,9},{9,5},{13,1},{2,14},{6,10},... | collective-permute-start | bytes 196616 | tf_op jit(solution)/shard_map/ppermute | solution.py:274
  6.7 1.5 %collective-permute-start.3 = (bf16[384,128]{1,0:T(8,128)(2,1)S(1)}, bf16[384,128]{1,0:T(8,128)(2,1)S(1)}, u32[]{:S(2)}, u32[]{:S(2)}) collective-permute-start(bf16[384,128]{1,0:T(8,128)(2,1)S(1)} %get-tuple-element.12.refs_1_), channel_id=1, source_target_pairs={{0,1},{1,0},{2,3},{3,2},{4,5},{5,4},{6,7},{7,6},{8,9},{9,8},{10,11... | collective-permute-start | bytes 294920 | tf_op jit(solution)/shard_map/ppermute | solution.py:276
  8.2 1.5 %collective-permute-start.5 = (bf16[384,128]{1,0:T(8,128)(2,1)S(1)}, bf16[384,128]{1,0:T(8,128)(2,1)S(1)}, u32[]{:S(2)}, u32[]{:S(2)}) collective-permute-start(bf16[384,128]{1,0:T(8,128)(2,1)S(1)} %get-tuple-element.12.refs_1_), channel_id=1, source_target_pairs={{0,2},{1,3},{2,0},{3,1},{4,6},{5,7},{6,4},{7,5},{8,10},{9,11},{10,... | collective-permute-start | bytes 294920 | tf_op jit(solution)/shard_map/ppermute | solution.py:276
  9.8 2.4 %collective-permute-start.7 = (bf16[384,128]{1,0:T(8,128)(2,1)S(1)}, bf16[384,128]{1,0:T(8,128)(2,1)S(1)}, u32[]{:S(2)}, u32[]{:S(2)}) collective-permute-start(bf16[384,128]{1,0:T(8,128)(2,1)S(1)} %get-tuple-element.12.refs_1_), channel_id=1, source_target_pairs={{0,3},{1,2},{2,1},{3,0},{4,7},{5,6},{6,5},{7,4},{8,11},{9,10},{10,... | collective-permute-start | bytes 294920 | tf_op jit(solution)/shard_map/ppermute | solution.py:276
  12.1 0.7 %collective-permute-done.1.refs_2_ = bf16[1,2,128,128]{3,2,1,0:T(8,128)(2,1)S(1)} collective-permute-done((bf16[1,2,128,128]{3,2,1,0:T(8,128)(2,1)S(1)}, bf16[1,2,128,128]{3,2,1,0:T(8,128)(2,1)S(1)}, u32[]{:S(2)}, u32[]{:S(2)}) %collective-permute-start.1) | collective-permute-done | bytes 65568 | tf_op jit(solution)/shard_map/ppermute | solution.py:274
  12.9 2.1 %collective-permute-start = (bf16[1,2,128,128]{3,2,1,0:T(8,128)(2,1)S(1)}, bf16[1,2,128,128]{3,2,1,0:T(8,128)(2,1)S(1)}, u32[]{:S(2)}, u32[]{:S(2)}) collective-permute-start(bf16[1,2,128,128]{3,2,1,0:T(8,128)(2,1)S(1)} %get-tuple-element.13.refs_0_), channel_id=1, source_target_pairs={{0,4},{4,0},{8,12},{12,8},{1,5},{5,1},{9,13},{13,9},{2,6},{6,2},{1... | collective-permute-start | bytes 196616 | tf_op jit(solution)/shard_map/ppermute | solution.py:274
  14.9 2.2 %collective-permute-done.refs_1_ = bf16[1,2,128,128]{3,2,1,0:T(8,128)(2,1)S(1)} collective-permute-done((bf16[1,2,128,128]{3,2,1,0:T(8,128)(2,1)S(1)}, bf16[1,2,128,128]{3,2,1,0:T(8,128)(2,1)S(1)}, u32[]{:S(2)}, u32[]{:S(2)}) %collective-permute-start) | collective-permute-done | bytes 65568 | tf_op jit(solution)/shard_map/ppermute | solution.py:274
  17.2 0.1 prepare.1
  17.3 0.6 %attend.3 = bf16[400,128]{1,0:T(8,128)(2,1)S(1)} custom-call(s32[16,128]{1,0:T(8,128)S(1)} %get-tuple-element.11.refs_0_, bf16[384,128]{1,0:T(8,128)(2,1)S(1)} %collective-permute-done.3.refs_1_, bf16[1,512,128]{2,1,0:T(8,128)(2,1)S(1)} %get-tuple-element.14.refs_2_, bf16[1,128,512]{2,1,0:T(8,128)(2,1)S(1)} %get-tuple-element.15.refs_3_), custom_call_target="tpu_custom_call" | custom-call | flops 100663296 | bytes 458752 | tf_op jit(solution)/shard_map/attend/pallas_call | solution.py:302
  17.9 1.5 %collective-permute-start.4 = (bf16[400,128]{1,0:T(8,128)(2,1)S(1)}, bf16[400,128]{1,0:T(8,128)(2,1)S(1)}, u32[]{:S(2)}, u32[]{:S(2)}) collective-permute-start(bf16[400,128]{1,0:T(8,128)(2,1)S(1)} %attend.3), channel_id=1, source_target_pairs={{1,0},{0,1},{3,2},{2,3},{5,4},{4,5},{7,6},{6,7},{9,8},{8,9},{11,10... | collective-permute-start | bytes 307208 | tf_op jit(solution)/shard_map/ppermute | solution.py:322
  19.4 0.6 %attend.4 = bf16[400,128]{1,0:T(8,128)(2,1)S(1)} custom-call(s32[16,128]{1,0:T(8,128)S(1)} %get-tuple-element.11.refs_0_, bf16[384,128]{1,0:T(8,128)(2,1)S(1)} %collective-permute-done.5.refs_1_, bf16[1,512,128]{2,1,0:T(8,128)(2,1)S(1)} %get-tuple-element.14.refs_2_, bf16[1,128,512]{2,1,0:T(8,128)(2,1)S(1)} %get-tuple-element.15.refs_3_), custom_call_target="tpu_custom_call" | custom-call | flops 100663296 | bytes 458752 | tf_op jit(solution)/shard_map/attend/pallas_call | solution.py:302
  20.1 1.6 %collective-permute-start.6 = (bf16[400,128]{1,0:T(8,128)(2,1)S(1)}, bf16[400,128]{1,0:T(8,128)(2,1)S(1)}, u32[]{:S(2)}, u32[]{:S(2)}) collective-permute-start(bf16[400,128]{1,0:T(8,128)(2,1)S(1)} %attend.4), channel_id=1, source_target_pairs={{2,0},{3,1},{0,2},{1,3},{6,4},{7,5},{4,6},{5,7},{10,8},{11,9},{8,1... | collective-permute-start | bytes 307208 | tf_op jit(solution)/shard_map/ppermute | solution.py:322
  21.7 0.6 %attend.5 = bf16[400,128]{1,0:T(8,128)(2,1)S(1)} custom-call(s32[16,128]{1,0:T(8,128)S(1)} %get-tuple-element.11.refs_0_, bf16[384,128]{1,0:T(8,128)(2,1)S(1)} %collective-permute-done.7.refs_1_, bf16[1,512,128]{2,1,0:T(8,128)(2,1)S(1)} %get-tuple-element.14.refs_2_, bf16[1,128,512]{2,1,0:T(8,128)(2,1)S(1)} %get-tuple-element.15.refs_3_), custom_call_target="tpu_custom_call" | custom-call | flops 100663296 | bytes 458752 | tf_op jit(solution)/shard_map/attend/pallas_call | solution.py:302
  22.3 0.6 %collective-permute-start.8 = (bf16[400,128]{1,0:T(8,128)(2,1)S(1)}, bf16[400,128]{1,0:T(8,128)(2,1)S(1)}, u32[]{:S(2)}, u32[]{:S(2)}) collective-permute-start(bf16[400,128]{1,0:T(8,128)(2,1)S(1)} %attend.5), channel_id=1, source_target_pairs={{3,0},{2,1},{1,2},{0,3},{7,4},{6,5},{5,6},{4,7},{11,8},{10,9},{9,1... | collective-permute-start | bytes 307208 | tf_op jit(solution)/shard_map/ppermute | solution.py:322
  22.9 1.9 %attend_fetch.1 = (bf16[400,128]{1,0:T(8,128)(2,1)S(1)}, bf16[384,1536]{1,0:T(8,128)(2,1)S(1)}) custom-call(s32[16,128]{1,0:T(8,128)S(1)} %get-tuple-element.11.refs_0_, bf16[384,128]{1,0:T(8,128)(2,1)S(1)} %get-tuple-element.12.refs_1_, bf16[1,512,128]{2,1,0:T(8,128)(2,1)S(1)} %get-tuple-element.14.refs_2_, ...), custom_call_target="tpu_custom_call" | custom-call | flops 100663296 | bytes 458752 | tf_op jit(solution)/shard_map/attend_fetch/pallas_call | solution.py:311
  24.8 1.1 %collective-permute-done.6.refs_2_ = bf16[400,128]{1,0:T(8,128)(2,1)S(1)} collective-permute-done((bf16[400,128]{1,0:T(8,128)(2,1)S(1)}, bf16[400,128]{1,0:T(8,128)(2,1)S(1)}, u32[]{:S(2)}, u32[]{:S(2)}) %collective-permute-start.6) | collective-permute-done | bytes 102432 | tf_op jit(solution)/shard_map/ppermute | solution.py:322
  25.9 2.0 %collective-permute-done.8.refs_3_ = bf16[400,128]{1,0:T(8,128)(2,1)S(1)} collective-permute-done((bf16[400,128]{1,0:T(8,128)(2,1)S(1)}, bf16[400,128]{1,0:T(8,128)(2,1)S(1)}, u32[]{:S(2)}, u32[]{:S(2)}) %collective-permute-start.8) | collective-permute-done | bytes 102432 | tf_op jit(solution)/shard_map/ppermute | solution.py:322
  27.9 0.1 combine.1
  28.0 0.1 collective-permute-start.9
  28.1 0.4 %project_home.1.home_ref = bf16[128,1536]{1,0:T(8,128)(2,1)S(1)} custom-call(bf16[384,128]{1,0:T(8,128)(2,1)S(1)} %get-tuple-element.17.attended_ref, bf16[384,1536]{1,0:T(8,128)(2,1)S(1)} %get-tuple-element.18.weight_ref), custom_call_target="tpu_custom_call" | custom-call | flops 150994944 | bytes 1179648 | tf_op jit(solution)/shard_map/project_home/pallas_call | solution.py:336
  28.5 0.9 %collective-permute-done.9.other_ref = bf16[384,128]{1,0:T(8,128)(2,1)S(1)} collective-permute-done((bf16[384,128]{1,0:T(8,128)(2,1)S(1)}, bf16[384,128]{1,0:T(8,128)(2,1)S(1)}, u32[]{:S(2)}, u32[]{:S(2)}) %collective-permute-start.9) | collective-permute-done | bytes 98336 | tf_op jit(solution)/shard_map/ppermute | solution.py:334
  29.4 1.1 %finish.1 = (bf16[128,1536]{1,0:T(8,128)(2,1)}, f32[3,128]{1,0:T(4,128)}) custom-call(bf16[128,1536]{1,0:T(8,128)(2,1)S(1)} %project_home.1.home_ref, bf16[384,128]{1,0:T(8,128)(2,1)S(1)} %collective-permute-done.9.other_ref, bf16[384,3072]{1,0:T(8,128)(2,1)S(1)} %collective-permute-done.10.weight_ref, f32[3,128]{1,0:T(4,128)S(1)} %get-tuple-element.19.log_ref), custom_call_target="tpu_custom_call" | custom-call | tf_op jit(solution)/shard_map/finish/pallas_call | solution.py:345
  (7 shorter events, 0.0 us)
Async XLA Ops:
  0.6 28.8 %collective-permute-start.10 = (bf16[384,3072]{1,0:T(8,128)(2,1)}, bf16[384,3072]{1,0:T(8,128)(2,1)S(1)}, u32[]{:S(2)}, u32[]{:S(2)}) collective-permute-start(bf16[384,3072]{1,0:T(8,128)(2,1)} %refs_4_.1), channel_id=1, source_target_pairs={{0,16},{16,0},{1,17},{17,1},{2,18},{18,2},{3,19},{19,3},{4,20},{20... | collective-permute-start | bytes 7077896 | tf_op jit(solution)/shard_map/ppermute | solution.py:277
  2.1 7.7 %collective-permute-start.2 = (bf16[1,2,128,128]{3,2,1,0:T(8,128)(2,1)S(1)}, bf16[1,2,128,128]{3,2,1,0:T(8,128)(2,1)S(1)}, u32[]{:S(2)}, u32[]{:S(2)}) collective-permute-start(bf16[1,2,128,128]{3,2,1,0:T(8,128)(2,1)S(1)} %get-tuple-element.13.refs_0_), channel_id=1, source_target_pairs={{0,12},{4,8},{8,4},{12,0},{1,13},{5,9},{9,5},{13,1},{2,14},{6,10},... | collective-permute-start | bytes 196616 | tf_op jit(solution)/shard_map/ppermute | solution.py:274
  6.7 6.1 %collective-permute-start.1 = (bf16[1,2,128,128]{3,2,1,0:T(8,128)(2,1)S(1)}, bf16[1,2,128,128]{3,2,1,0:T(8,128)(2,1)S(1)}, u32[]{:S(2)}, u32[]{:S(2)}) collective-permute-start(bf16[1,2,128,128]{3,2,1,0:T(8,128)(2,1)S(1)} %get-tuple-element.13.refs_0_), channel_id=1, source_target_pairs={{0,8},{4,12},{8,0},{12,4},{1,9},{5,13},{9,1},{13,5},{2,10},{6,14},... | collective-permute-start | bytes 196616 | tf_op jit(solution)/shard_map/ppermute | solution.py:274
  6.7 10.5 %collective-permute-start.3 = (bf16[384,128]{1,0:T(8,128)(2,1)S(1)}, bf16[384,128]{1,0:T(8,128)(2,1)S(1)}, u32[]{:S(2)}, u32[]{:S(2)}) collective-permute-start(bf16[384,128]{1,0:T(8,128)(2,1)S(1)} %get-tuple-element.12.refs_1_), channel_id=1, source_target_pairs={{0,1},{1,0},{2,3},{3,2},{4,5},{5,4},{6,7},{7,6},{8,9},{9,8},{10,11... | collective-permute-start | bytes 294920 | tf_op jit(solution)/shard_map/ppermute | solution.py:276
  8.2 11.2 %collective-permute-start.5 = (bf16[384,128]{1,0:T(8,128)(2,1)S(1)}, bf16[384,128]{1,0:T(8,128)(2,1)S(1)}, u32[]{:S(2)}, u32[]{:S(2)}) collective-permute-start(bf16[384,128]{1,0:T(8,128)(2,1)S(1)} %get-tuple-element.12.refs_1_), channel_id=1, source_target_pairs={{0,2},{1,3},{2,0},{3,1},{4,6},{5,7},{6,4},{7,5},{8,10},{9,11},{10,... | collective-permute-start | bytes 294920 | tf_op jit(solution)/shard_map/ppermute | solution.py:276
  9.8 11.9 %collective-permute-start.7 = (bf16[384,128]{1,0:T(8,128)(2,1)S(1)}, bf16[384,128]{1,0:T(8,128)(2,1)S(1)}, u32[]{:S(2)}, u32[]{:S(2)}) collective-permute-start(bf16[384,128]{1,0:T(8,128)(2,1)S(1)} %get-tuple-element.12.refs_1_), channel_id=1, source_target_pairs={{0,3},{1,2},{2,1},{3,0},{4,7},{5,6},{6,5},{7,4},{8,11},{9,10},{10,... | collective-permute-start | bytes 294920 | tf_op jit(solution)/shard_map/ppermute | solution.py:276
  12.9 4.3 %collective-permute-start = (bf16[1,2,128,128]{3,2,1,0:T(8,128)(2,1)S(1)}, bf16[1,2,128,128]{3,2,1,0:T(8,128)(2,1)S(1)}, u32[]{:S(2)}, u32[]{:S(2)}) collective-permute-start(bf16[1,2,128,128]{3,2,1,0:T(8,128)(2,1)S(1)} %get-tuple-element.13.refs_0_), channel_id=1, source_target_pairs={{0,4},{4,0},{8,12},{12,8},{1,5},{5,1},{9,13},{13,9},{2,6},{6,2},{1... | collective-permute-start | bytes 196616 | tf_op jit(solution)/shard_map/ppermute | solution.py:274
  17.9 6.8 %collective-permute-start.4 = (bf16[400,128]{1,0:T(8,128)(2,1)S(1)}, bf16[400,128]{1,0:T(8,128)(2,1)S(1)}, u32[]{:S(2)}, u32[]{:S(2)}) collective-permute-start(bf16[400,128]{1,0:T(8,128)(2,1)S(1)} %attend.3), channel_id=1, source_target_pairs={{1,0},{0,1},{3,2},{2,3},{5,4},{4,5},{7,6},{6,7},{9,8},{8,9},{11,10... | collective-permute-start | bytes 307208 | tf_op jit(solution)/shard_map/ppermute | solution.py:322
  20.1 5.8 %collective-permute-start.6 = (bf16[400,128]{1,0:T(8,128)(2,1)S(1)}, bf16[400,128]{1,0:T(8,128)(2,1)S(1)}, u32[]{:S(2)}, u32[]{:S(2)}) collective-permute-start(bf16[400,128]{1,0:T(8,128)(2,1)S(1)} %attend.4), channel_id=1, source_target_pairs={{2,0},{3,1},{0,2},{1,3},{6,4},{7,5},{4,6},{5,7},{10,8},{11,9},{8,1... | collective-permute-start | bytes 307208 | tf_op jit(solution)/shard_map/ppermute | solution.py:322
  22.3 5.6 %collective-permute-start.8 = (bf16[400,128]{1,0:T(8,128)(2,1)S(1)}, bf16[400,128]{1,0:T(8,128)(2,1)S(1)}, u32[]{:S(2)}, u32[]{:S(2)}) collective-permute-start(bf16[400,128]{1,0:T(8,128)(2,1)S(1)} %attend.5), channel_id=1, source_target_pairs={{3,0},{2,1},{1,2},{0,3},{7,4},{6,5},{5,6},{4,7},{11,8},{10,9},{9,1... | collective-permute-start | bytes 307208 | tf_op jit(solution)/shard_map/ppermute | solution.py:322
  28.0 1.4 %collective-permute-start.9 = (bf16[384,128]{1,0:T(8,128)(2,1)S(1)}, bf16[384,128]{1,0:T(8,128)(2,1)S(1)}, u32[]{:S(2)}, u32[]{:S(2)}) collective-permute-start(bf16[384,128]{1,0:T(8,128)(2,1)S(1)} %get-tuple-element.17.attended_ref), channel_id=1, source_target_pairs={{0,16},{16,0},{1,17},{17,1},{2,18},{18,2},{3,19},{19,3},{4,20},{20... | collective-permute-start | bytes 294920 | tf_op jit(solution)/shard_map/ppermute | solution.py:334
